TPU v7x, 128 devices: a whole 4x4x4 slice. The times are simulated.
128 devices in a mesh: rows: 8 (over y, core), cols: 16 (over z, x).
Axes of the slice: x: 4, y: 4, z: 4, core: 2. Of those that a mesh axis runs over, the one named last changes fastest.
Arguments:
- image: bfloat16 [256, 1024, 128], P('rows', 'cols'), may hold values from -6 to 6
- routes: int32 [32, 128, 4], P('rows', 'cols'), may hold values from 0 to 4095, as said below
- norm_gain: float32 [128], replicated, may hold values from 0.1 to 1.9
- qkv_weight: bfloat16 [128, 384], replicated, may hold values from -25.455844 to 25.455844
- lce_weight: float32 [5, 5, 128], replicated, may hold values from -1.25 to 1.25
- out_weight: bfloat16 [128, 128], replicated, may hold values from -0.5 to 0.5
- mlp_gain: float32 [128], replicated, may hold values from 0.1 to 1.9
- up_weight: bfloat16 [128, 384], replicated, may hold values from -0.5 to 0.5
- down_weight: bfloat16 [384, 128], replicated, may hold values from -0.3125 to 0.3125
Outputs:
- refined: bfloat16 [256, 1024, 128], P('rows', 'cols')
Inputs may be any that keep to these rules, and one draw needn't show every extreme that they name: Each region names 4 different regions. Of the routes of the regions of one device, at most 2 lead to the regions of any one device, and in every draw some device receives exactly 2 from every device.
All inputs are finite; a program needn't handle non-finite values.
Results may differ from a plain program's by a relative error of at most 0.0038.
The roundings to bfloat16 on the way count: a program that leaves them out, or rounds other values in their place, can miss the bound.
Values may be sent and summed in bfloat16 or wider, within the bound.
A program may use at most 128 MiB of HBM per device.

v0:
```python
import math

import jax
import jax.numpy as jnp
from jax import lax
from jax.sharding import PartitionSpec as P

HEADS = 4


EPSILON = 1e-06


def cut_along(shard, dim, length):
    before, after = (shard.shape[:dim], shard.shape[dim + 1 :])
    return jnp.moveaxis(shard.reshape(*before, length, -1, *after), dim, 0)


def joined_along(pieces, dim):
    dims = list(pieces.shape[1:])
    dims[dim] *= pieces.shape[0]
    return jnp.moveaxis(pieces, 0, dim).reshape(dims)


def one_exchange(shard, axis, axes, splits, concats):
    sizes = [lax.axis_size(a) for a in axes]
    pieces = cut_along(shard, splits[0], sizes[0])
    pieces = jnp.moveaxis(cut_along(pieces, splits[1] + 1, sizes[1]), 0, 1)
    inside = pieces.shape[2:]
    pieces = pieces.reshape(-1, *inside)
    pieces = lax.all_to_all(pieces, axis, split_axis=0, concat_axis=0, tiled=True)
    pieces = joined_along(pieces.reshape(*sizes, *inside), concats[0] + 1)
    return joined_along(pieces, concats[1])


def padded_2(block, sides, width):
    for axis, dim in sides:
        count = lax.axis_size(axis)
        forward = [(i, i + 1) for i in range(count - 1)]
        backward = [(target, source) for source, target in forward]
        low = lax.ppermute(
            lax.slice_in_dim(block, block.shape[dim] - width, None, axis=dim), axis, forward
        )
        high = lax.ppermute(lax.slice_in_dim(block, 0, width, axis=dim), axis, backward)
        block = jnp.concatenate([low, block, high], axis=dim)
    return block


def layer_norm(values, norm_scale):
    floats = values.astype(jnp.float32)
    centered = floats - jnp.mean(floats, axis=-1, keepdims=True)
    spread = jnp.mean(centered * centered, axis=-1, keepdims=True)
    return centered * lax.rsqrt(spread + EPSILON) * norm_scale


def to_regions(grid_field, region_side):
    height, grid_width, channels = grid_field.shape
    shaped = grid_field.reshape(
        height // region_side, region_side, grid_width // region_side, region_side, channels
    )
    return shaped.transpose(0, 2, 1, 3, 4).reshape(-1, region_side * region_side, channels)


def from_regions(blocks, region_side, height, grid_width):
    channels = blocks.shape[-1]
    shaped = blocks.reshape(
        height // region_side, grid_width // region_side, region_side, region_side, channels
    )
    return shaped.transpose(0, 2, 1, 3, 4).reshape(height, grid_width, channels)


def region_attention(queries, keyvals, head_count):
    group_count, length, channels = queries.shape
    head_size = channels // head_count
    q_heads = queries.reshape(group_count, length, head_count, head_size)
    k_heads = keyvals[..., :channels].reshape(group_count, -1, head_count, head_size)
    v_heads = keyvals[..., channels:].reshape(group_count, -1, head_count, head_size)
    scores = jnp.einsum(
        "gqhd,gkhd->ghqk", q_heads, k_heads, preferred_element_type=jnp.float32
    ) * head_size ** (-0.5)
    row_max = jnp.max(scores, axis=-1, keepdims=True)
    expons = jnp.exp(scores - row_max)
    weights = (expons / jnp.sum(expons, axis=-1, keepdims=True)).astype(jnp.bfloat16)
    blended = jnp.einsum("ghqk,gkhd->gqhd", weights, v_heads, preferred_element_type=jnp.float32)
    return blended.reshape(group_count, length, channels)


def local_context(padded, kernel, height, grid_width):
    kernel_size = kernel.shape[0]
    summed = jnp.zeros((height, grid_width, padded.shape[-1]), jnp.float32)
    for offset_row in range(kernel_size):
        for offset_col in range(kernel_size):
            window = padded[
                offset_row : offset_row + height, offset_col : offset_col + grid_width
            ].astype(jnp.float32)
            summed = summed + window * kernel[offset_row, offset_col]
    return summed


def body(
    image, routes, norm_gain, qkv_weight, lce_weight, out_weight, mlp_gain, up_weight, down_weight
):
    height, grid_width, channels = image.shape
    row_devices = lax.axis_size("rows")
    col_devices = lax.axis_size("cols")
    devices = row_devices * col_devices
    region_rows, region_cols, pick_count = routes.shape
    region_side = height // region_rows
    region_count = region_rows * region_cols
    region_area = region_side * region_side
    pair_count = region_count * pick_count
    capacity = max(2, 2 * pair_count // devices)
    all_cols = region_cols * col_devices
    normed = layer_norm(image, norm_gain).astype(jnp.bfloat16)
    projected = jnp.dot(
        normed.reshape(-1, channels), qkv_weight, preferred_element_type=jnp.float32
    )
    projected = projected.astype(jnp.bfloat16).reshape(height, grid_width, 3 * channels)
    queries = to_regions(projected[..., :channels], region_side)
    keyvals = to_regions(projected[..., channels:], region_side)
    values = projected[..., 2 * channels :]
    targets = routes.reshape(pair_count)
    target_row = targets // all_cols
    target_col = targets % all_cols
    owners = target_row // region_rows * col_devices + target_col // region_cols
    local_index = target_row % region_rows * region_cols + target_col % region_cols
    one_hot = (owners[:, None] == jnp.arange(devices, dtype=jnp.int32)[None, :]).astype(jnp.int32)
    before = jnp.cumsum(one_hot, axis=0) - one_hot
    slot_index = jnp.sum(before * one_hot, axis=1)
    position = owners * capacity + slot_index
    requests = jnp.zeros((devices * capacity,), jnp.int32).at[position].set(local_index)
    requested = one_exchange(
        requests.reshape(row_devices, col_devices, capacity),
        ("rows", "cols"),
        ("rows", "cols"),
        (0, 1),
        (0, 1),
    )
    served = keyvals[requested.reshape(-1)].reshape(
        row_devices, col_devices, capacity, region_area, 2 * channels
    )
    returned = one_exchange(served, ("rows", "cols"), ("rows", "cols"), (0, 1), (0, 1))
    margin = (lce_weight.shape[0] - 1) // 2
    padded = padded_2(values, (("rows", 0), ("cols", 1)), margin)
    context = local_context(padded, lce_weight, height, grid_width)
    fetched = returned.reshape(devices * capacity, region_area, 2 * channels)[position]
    fetched = fetched.reshape(region_count, pick_count * region_area, 2 * channels)
    group_size = math.gcd(region_count, 8)
    group_count = region_count // group_size

    def attend(inputs):
        return region_attention(inputs[0], inputs[1], HEADS)

    blended = lax.map(
        attend,
        (
            queries.reshape(group_count, group_size, region_area, channels),
            fetched.reshape(group_count, group_size, pick_count * region_area, 2 * channels),
        ),
    )
    attended = from_regions(
        blended.reshape(region_count, region_area, channels), region_side, height, grid_width
    )
    combined = (attended + context).astype(jnp.bfloat16)
    projected_out = jnp.dot(
        combined.reshape(-1, channels), out_weight, preferred_element_type=jnp.float32
    )
    residual = image.astype(jnp.float32) + projected_out.reshape(height, grid_width, channels)
    stored = lax.optimization_barrier(residual.astype(jnp.bfloat16))
    second = layer_norm(stored, mlp_gain).astype(jnp.bfloat16)
    hidden = jax.nn.gelu(
        jnp.dot(second.reshape(-1, channels), up_weight, preferred_element_type=jnp.float32),
        approximate=True,
    ).astype(jnp.bfloat16)
    lowered = jnp.dot(hidden, down_weight, preferred_element_type=jnp.float32).reshape(
        height, grid_width, channels
    )
    return (stored.astype(jnp.float32) + lowered).astype(jnp.bfloat16)


def solution(mesh):
    in_specs = (P("rows", "cols", None), P("rows", "cols", None), P(), P(), P(), P(), P(), P(), P())
    out_specs = P("rows", "cols", None)
    return jax.shard_map(body, mesh=mesh, in_specs=in_specs, out_specs=out_specs, check_vma=False)
```

profile of v0, /device:TPU:1, one launch (start us, length us, event | category | flops | bytes accessed | tf_op | source)
XLA Modules:
  0.0 194.4 jit_solution(13709962111181587537)
XLA Ops:
  0.0 0.8 copy.28
  1.6 1.0 scatter_custom_fusion
  2.5 0.8 reshape_transpose_transpose_reshape_reshape_reshape.6
  3.3 11.5 %all-to-all-start = ((s32[128,1,1,2]{3,2,1,0:T(1,128)}), s32[128,1,1,2]{3,2,1,0:T(1,128)S(1)}, u32[]{:S(2)}, u32[]{:S(2)}) async-start(s32[128,1,1,2]{3,2,1,0:T(1,128)} %bitcast.13), calls=%async_computation | async-start | bytes 131072 | tf_op jit(solution)/shard_map/all_to_all | solution.py:31
  14.8 1.4 convert_reduce_fusion.1
  16.2 1.7 fusion.24
  17.9 1.7 fusion.26
  20.4 4.2 %all-to-all-done = s32[128,1,1,2]{3,2,1,0:T(1,128)S(1)} async-done(((s32[128,1,1,2]{3,2,1,0:T(1,128)}), s32[128,1,1,2]{3,2,1,0:T(1,128)S(1)}, u32[]{:S(2)}, u32[]{:S(2)}) %all-to-all-start) | async-done | bytes 1056 | tf_op jit(solution)/shard_map/all_to_all | solution.py:31
  24.7 8.5 %gather_fusion = bf16[256,64,256]{2,1,0:T(8,128)(2,1)} fusion(bf16[32,64,256]{2,1,0:T(8,128)(2,1)S(1)} %bitcast.135, s32[1024]{0:T(1024)S(1)} %pad_clamp_fusion.1), kind=kCustom, calls=%fused_computation | custom fusion | bytes 16778240 | tf_op jit(solution)/shard_map/gather | solution.py:139
  33.2 6.1 %all-to-all-start.1 = ((bf16[128,1,1,2,64,256]{5,4,3,2,1,0:T(8,128)(2,1)}), bf16[128,1,1,2,64,256]{5,4,3,2,1,0:T(8,128)(2,1)}, u32[]{:S(2)}, u32[]{:S(2)}) async-start(bf16[128,1,1,2,64,256]{5,4,3,2,1,0:T(8,128)(2,1)} %bitcast.137), calls=%async_computation.1 | async-start | bytes 16777216 | tf_op jit(solution)/shard_map/all_to_all | solution.py:31
  39.3 3.5 %collective-permute-start = (bf16[2,64,128]{2,1,0:T(8,128)(2,1)S(1)}, bf16[2,64,128]{2,1,0:T(8,128)(2,1)S(1)}, u32[]{:S(2)}, u32[]{:S(2)}) collective-permute-start(bf16[2,64,128]{2,1,0:T(8,128)(2,1)S(1)} %get-tuple-element.56), channel_id=1, source_target_pairs={{0,16},{16,32},{32,48},{48,64},{64,80},{80,96},{96,112},{1,17},{17... | collective-permute-start | bytes 98312 | tf_op jit(solution)/shard_map/ppermute | solution.py:41
  42.8 1.9 collective-permute-start.1
  44.8 0.7 slice_bitcast_fusion.24
  45.8 0.6 slice_bitcast_fusion.23
  46.4 86.7 %collective-permute-done = bf16[2,64,128]{2,1,0:T(8,128)(2,1)S(1)} collective-permute-done((bf16[2,64,128]{2,1,0:T(8,128)(2,1)S(1)}, bf16[2,64,128]{2,1,0:T(8,128)(2,1)S(1)}, u32[]{:S(2)}, u32[]{:S(2)}) %collective-permute-start) | collective-permute-done | bytes 32800 | tf_op jit(solution)/shard_map/ppermute | solution.py:41
  133.1 1.3 collective-permute-done.1
  134.5 10.8 %collective-permute-start.2 = (bf16[36,2,128]{2,1,0:T(2,128)(2,1)S(1)}, bf16[36,2,128]{2,1,0:T(2,128)(2,1)S(1)}, u32[]{:S(2)}, u32[]{:S(2)}) collective-permute-start(bf16[36,2,128]{2,1,0:T(2,128)(2,1)S(1)} %get-tuple-element.62), channel_id=1, source_target_pairs={{0,1},{1,2},{2,3},{3,4},{4,5},{5,6},{6,7},{7,8},{8,9},{9,10},{10,1... | collective-permute-start | bytes 55304 | tf_op jit(solution)/shard_map/ppermute | solution.py:41
  145.3 1.5 collective-permute-start.3
  146.8 0.9 copy.46
  147.7 2.1 %collective-permute-done.3 = bf16[36,2,128]{2,1,0:T(2,128)(2,1)S(1)} collective-permute-done((bf16[36,2,128]{2,1,0:T(2,128)(2,1)S(1)}, bf16[36,2,128]{2,1,0:T(2,128)(2,1)S(1)}, u32[]{:S(2)}, u32[]{:S(2)}) %collective-permute-start.3) | collective-permute-done | bytes 18464 | tf_op jit(solution)/shard_map/ppermute | solution.py:44
  149.8 1.4 maximum_maximum_fusion
  151.2 6.2 %gather_fusion.1 = bf16[128,64,256]{2,1,0:T(8,128)(2,1)} fusion(bf16[256,64,256]{2,1,0:T(8,128)(2,1)} %bitcast.25, s32[1024]{0:T(1024)S(1)} %pad_clamp_fusion), kind=kCustom, calls=%fused_computation.1 | custom fusion | bytes 8389120 | tf_op jit(solution)/shard_map/gather | solution.py:146
  157.4 22.9 %while.10 = (s32[]{:T(128)}, f32[4,8,64,128]{3,2,1,0:T(8,128)}, bf16[4,8,256,256]{3,2,1,0:T(8,128)(2,1)}, bf16[4,8,64,128]{3,2,1,0:T(8,128)(2,1)}, s32[]{:T(128)}) while((s32[]{:T(128)}, f32[4,8,64,128]{3,2,1,0:T(8,128)}, bf16[4,8,256,256]{3,2,1,0:T(8,128)(2,1)}, bf16[4,8,64,128]{3,2,1,0:T(8,128)(2,1)}, s32[]{:T(128)}) %tuple.60), condition=%wide.region_8.9_spmd, body=%wide.region_5.8_spmd.sunk | while | flops 69730560 | bytes 13517381 | solution.py:154
  157.4 1.3 constant_dynamic-slice_fusion.4
  159.3 0.9 constant_dynamic-slice_fusion.5
  160.4 1.0 fusion.64
  161.5 0.7 fusion.65
  162.4 0.7 constant_dynamic-update-slice_fusion.2
  163.1 1.3 constant_dynamic-slice_fusion.4
  165.1 0.9 constant_dynamic-slice_fusion.5
  166.2 1.0 fusion.64
  167.2 0.7 fusion.65
  168.1 0.7 constant_dynamic-update-slice_fusion.2
  168.8 1.3 constant_dynamic-slice_fusion.4
  170.8 0.9 constant_dynamic-slice_fusion.5
  171.9 1.0 fusion.64
  172.9 0.7 fusion.65
  173.8 0.7 constant_dynamic-update-slice_fusion.2
  174.6 1.3 constant_dynamic-slice_fusion.4
  176.5 0.9 constant_dynamic-slice_fusion.5
  177.6 1.0 fusion.64
  178.6 0.7 fusion.65
  179.6 0.7 constant_dynamic-update-slice_fusion.2
  180.6 1.5 copy.36
  182.4 8.1 %fusion.16 = bf16[32,64,128]{2,1,0:T(8,128)(2,1)S(1)} fusion(bf16[32,64,128]{2,1,0:T(8,128)(2,1)S(1)} %copy-done.1, f32[32,64,128]{2,1,0:T(8,128)S(1)} %bitcast.148, bf16[32,64,128]{2,1,0:T(8,128)(2,1)S(1)} %copy-done.3, bf16[2,64,128]{2,1,0:T(8,128)(2,1)S(1)} %copy-done.6, bf16[2,64,128]{2,1,0:T(8,128)(2,1)S(1)} %collective-permute-done, ...), kind=kOutput, calls=%fused_computation.32 | convolution fusion | flops 88866816 | bytes 13218304 | tf_op jit(solution)/shard_map/dot_general | solution.py:165
  190.8 0.6 fusion.21
  192.2 1.3 fusion.15
  193.5 0.9 fusion.27
  (117 shorter events, 7.0 us)
Async XLA Ops:
  0.0 19.6 %copy-start = (bf16[128,384]{1,0:T(8,128)(2,1)S(1)}, bf16[128,384]{1,0:T(8,128)(2,1)}, u32[]{:S(2)}) copy-start(bf16[128,384]{1,0:T(8,128)(2,1)} %param.14) | copy-start | bytes 294916
  3.3 21.2 %all-to-all-start = ((s32[128,1,1,2]{3,2,1,0:T(1,128)}), s32[128,1,1,2]{3,2,1,0:T(1,128)S(1)}, u32[]{:S(2)}, u32[]{:S(2)}) async-start(s32[128,1,1,2]{3,2,1,0:T(1,128)} %bitcast.13), calls=%async_computation | async-start | bytes 131072 | tf_op jit(solution)/shard_map/all_to_all | solution.py:31
  33.2 11.6 %copy-start.7 = (f32[5,5,128]{2,1,0:T(8,128)S(1)}, f32[5,5,128]{2,1,0:T(8,128)}, u32[]{:S(2)}) copy-start(f32[5,5,128]{2,1,0:T(8,128)} %param.15) | copy-start | bytes 38404
  33.2 118.0 %all-to-all-start.1 = ((bf16[128,1,1,2,64,256]{5,4,3,2,1,0:T(8,128)(2,1)}), bf16[128,1,1,2,64,256]{5,4,3,2,1,0:T(8,128)(2,1)}, u32[]{:S(2)}, u32[]{:S(2)}) async-start(bf16[128,1,1,2,64,256]{5,4,3,2,1,0:T(8,128)(2,1)} %bitcast.137), calls=%async_computation.1 | async-start | bytes 16777216 | tf_op jit(solution)/shard_map/all_to_all | solution.py:31
  39.3 93.9 %collective-permute-start = (bf16[2,64,128]{2,1,0:T(8,128)(2,1)S(1)}, bf16[2,64,128]{2,1,0:T(8,128)(2,1)S(1)}, u32[]{:S(2)}, u32[]{:S(2)}) collective-permute-start(bf16[2,64,128]{2,1,0:T(8,128)(2,1)S(1)} %get-tuple-element.56), channel_id=1, source_target_pairs={{0,16},{16,32},{32,48},{48,64},{64,80},{80,96},{96,112},{1,17},{17... | collective-permute-start | bytes 98312 | tf_op jit(solution)/shard_map/ppermute | solution.py:41
  42.8 91.6 %collective-permute-start.1 = (bf16[2,64,128]{2,1,0:T(8,128)(2,1)S(1)}, bf16[2,64,128]{2,1,0:T(8,128)(2,1)S(1)}, u32[]{:S(2)}, u32[]{:S(2)}) collective-permute-start(bf16[2,64,128]{2,1,0:T(8,128)(2,1)S(1)} %get-tuple-element.57), channel_id=1, source_target_pairs={{16,0},{32,16},{48,32},{64,48},{80,64},{96,80},{112,96},{17,1},{33... | collective-permute-start | bytes 98312 | tf_op jit(solution)/shard_map/ppermute | solution.py:44
  45.7 111.7 %copy-start.2 = (bf16[32,64,128]{2,1,0:T(8,128)(2,1)}, bf16[32,64,128]{2,1,0:T(8,128)(2,1)S(1)}, u32[]{:S(2)}) copy-start(bf16[32,64,128]{2,1,0:T(8,128)(2,1)S(1)} %get-tuple-element.58) | copy-start | bytes 1572868
  134.4 23.0 %copy-start.5 = (bf16[2,64,128]{2,1,0:T(8,128)(2,1)}, bf16[2,64,128]{2,1,0:T(8,128)(2,1)S(1)}, u32[]{:S(2)}) copy-start(bf16[2,64,128]{2,1,0:T(8,128)(2,1)S(1)} %collective-permute-done.1) | copy-start | bytes 98308
  134.5 13.2 %collective-permute-start.2 = (bf16[36,2,128]{2,1,0:T(2,128)(2,1)S(1)}, bf16[36,2,128]{2,1,0:T(2,128)(2,1)S(1)}, u32[]{:S(2)}, u32[]{:S(2)}) collective-permute-start(bf16[36,2,128]{2,1,0:T(2,128)(2,1)S(1)} %get-tuple-element.62), channel_id=1, source_target_pairs={{0,1},{1,2},{2,3},{3,4},{4,5},{5,6},{6,7},{7,8},{8,9},{9,10},{10,1... | collective-permute-start | bytes 55304 | tf_op jit(solution)/shard_map/ppermute | solution.py:41
  145.3 4.5 %collective-permute-start.3 = (bf16[36,2,128]{2,1,0:T(2,128)(2,1)S(1)}, bf16[36,2,128]{2,1,0:T(2,128)(2,1)S(1)}, u32[]{:S(2)}, u32[]{:S(2)}) collective-permute-start(bf16[36,2,128]{2,1,0:T(2,128)(2,1)S(1)} %get-tuple-element.63), channel_id=1, source_target_pairs={{1,0},{2,1},{3,2},{4,3},{5,4},{6,5},{7,6},{8,7},{9,8},{10,9},{11,1... | collective-permute-start | bytes 55304 | tf_op jit(solution)/shard_map/ppermute | solution.py:44
  180.3 1.8 copy-start.1
  180.3 1.8 copy-start.3
  180.3 1.8 copy-start.4
  180.3 1.8 copy-start.6
  180.3 1.8 copy-start.9
  180.3 1.8 copy-start.10
  180.3 1.8 copy-start.11
  180.3 1.8 copy-start.12
  180.4 1.8 copy-start.13
  180.4 1.8 copy-start.14
  180.4 1.8 copy-start.15
  180.4 1.8 copy-start.16
  180.4 1.8 copy-start.17
  180.4 1.8 copy-start.18
  180.4 1.8 copy-start.19
  180.4 1.8 copy-start.20
  180.4 1.8 copy-start.21
  180.4 1.8 copy-start.22
  180.5 1.8 copy-start.23
  180.5 1.8 copy-start.24
  180.5 1.8 copy-start.25
  180.5 1.8 copy-start.26
  180.5 1.8 copy-start.27
  180.5 1.8 copy-start.28
  180.5 1.8 copy-start.29
  180.5 1.8 copy-start.30
  180.5 1.8 copy-start.31
  180.5 1.8 copy-start.32
  180.6 1.8 copy-start.33
  180.6 1.8 copy-start.36
  182.4 9.2 %copy-start.8 = (f32[128]{0:T(128)S(1)}, f32[128]{0:T(128)}, u32[]{:S(2)}) copy-start(f32[128]{0:T(128)} %param.17) | copy-start | bytes 1540
  190.5 1.7 copy-start.34
  190.5 1.7 copy-start.35
where the time goes:
time: 196 us; the launch traced here: 194 us
  waiting for transfers between devices  94.3 us (48%)
  local copies, waits for them, and re-layouts  37.6 us (19%)
  starting transfers between devices  35.3 us (18%)
  matrix products  17 us (9%)
  other arithmetic  9.26 us (5%)
    ppermute x2, waiting for transfers between devices, padded_2(): lax.ppermute(lax.slice_in_dim(block, block.shape[dim] - width, None, axis...  86.7 us
    all_to_all x2, starting transfers between devices, one_exchange(): lax.all_to_all(pieces, axis, split_axis=0, concat_axis=0, tiled=True)  17.6 us
    ppermute x2, starting transfers between devices, padded_2(): lax.ppermute(lax.slice_in_dim(block, block.shape[dim] - width, None, axis...  14.3 us
    dynamic_slice x16, local copies, waits for them, and re-layouts, body(): lax.map(attend, (queries.reshape(group_count, group_size, region_area, ch...  11.7 us
    gather x1, local copies, waits for them, and re-layouts, body(): keyvals[requested.reshape(-1)]  8.47 us
    dot_general x1, matrix products, body(): jnp.dot(combined.reshape(-1, channels), out_weight, preferred_element_typ...  8.09 us
    gather x1, local copies, waits for them, and re-layouts, body(): returned.reshape(devices * capacity, region_area, 2 * channels)[position]  6.18 us
    all_to_all x2, waiting for transfers between devices, one_exchange(): lax.all_to_all(pieces, axis, split_axis=0, concat_axis=0, tiled=True)  4.19 us
  transfers between devices with their start and end apart: 6, of which 4 were waited for; matrix products, arithmetic and copies ran while one was open for 5% of the time, Pallas kernels for 0%

commit v1 on v0

v1 whole, which is shorter than its diff:
```python
import functools
import itertools
import math

import jax
import jax.numpy as jnp
from jax import lax
from jax.experimental import pallas as pl
from jax.experimental.pallas import tpu as pltpu
from jax.sharding import PartitionSpec as P

MESH = pl.DeviceIdType.MESH
HEADS = 4
EPSILON = 1e-06
BIG = 1 << 20


def hops(offset):
    return sum(min(step, 4 - step) for step in offset[1:])


OFFSETS = sorted(
    (o for o in itertools.product(range(2), range(4), range(4), range(4)) if any(o)), key=hops
)


def layer_norm(floats, gain):
    centered = floats - jnp.mean(floats, axis=-1, keepdims=True)
    spread = jnp.mean(centered * centered, axis=-1, keepdims=True)
    return centered * lax.rsqrt(spread + EPSILON) * gain


def owner_of(route):
    return ((route >> 9) << 4) | ((route >> 3) & 15)


def local_of(route):
    return (((route >> 7) & 3) << 3) | (route & 7)


def to_strip(blocks):
    return blocks.reshape(8, 8, 8, 128).transpose(1, 0, 2, 3).reshape(8, 64, 128)


def exchange_kernel(
    routes_ref, image_ref, gain_ref, qkv_ref, lce_ref,
    recv_ref, q_ref, ctx_ref, pos_ref,
    normed, send, my_routes, all_routes, slots, slots_smem, grid_v, padded,
    route_send, route_recv, halo_send, halo_recv, data_send, data_recv, local_sem,
):
    row, col = lax.axis_index("rows"), lax.axis_index("cols")
    chip_y, core = row // 2, row % 2
    chip_z, chip_x = col // 4, col % 4
    me = row * 16 + col

    def peer(offset):
        dc, dy, dz, dx = offset
        return (
            (chip_y + dy) % 4 * 2 + (core + dc) % 2,
            (chip_z + dz) % 4 * 4 + (chip_x + dx) % 4,
        )

    barrier = pltpu.get_barrier_semaphore()
    for offset in reversed(OFFSETS):
        pl.semaphore_signal(barrier, inc=1, device_id=peer(offset), device_id_type=MESH)

    mine = jnp.concatenate(
        [routes_ref[i, t : t + 1, :] for i in range(4) for t in range(4)], axis=1
    )
    my_routes[...] = mine
    all_routes[pl.ds(me, 1), :] = mine

    lanes = lax.broadcasted_iota(jnp.int32, (128, 128), 1)
    subs = lax.broadcasted_iota(jnp.int32, (128, 128), 0)
    owners = jnp.broadcast_to(owner_of(mine), (128, 128))
    same = jnp.logical_and(owners == owners.T, subs < lanes)
    second = jnp.max(jnp.where(same, 1, 0), axis=0, keepdims=True)
    pos_ref[...] = owner_of(mine) * 2 + second

    gain = gain_ref[...]
    for i in range(4):
        strip = image_ref[pl.ds(8 * i, 8)].astype(jnp.float32)
        strip = to_strip(layer_norm(strip, gain)).astype(jnp.bfloat16)
        normed[pl.ds(8 * i, 8)] = strip
        projected = jnp.dot(
            strip.reshape(512, 128), qkv_ref[...], preferred_element_type=jnp.float32
        )
        q_ref[pl.ds(8 * i, 8)] = projected[:, :128].astype(jnp.bfloat16).reshape(8, 64, 128)
        values = projected[:, 256:].reshape(8, 8, 8, 128).transpose(1, 0, 2, 3)
        grid_v[pl.ds(2 + 8 * i, 8), pl.ds(1, 8)] = values.astype(jnp.bfloat16)

    pl.semaphore_wait(barrier, len(OFFSETS))

    route_copies = []
    for n, offset in enumerate(OFFSETS[::-1]):
        route_copies.append(
            pltpu.make_async_remote_copy(
                src_ref=my_routes,
                dst_ref=all_routes.at[pl.ds(me, 1)],
                send_sem=route_send.at[n],
                recv_sem=route_recv.at[n],
                device_id=peer(offset),
                device_id_type=MESH,
            )
        )
        route_copies[-1].start()

    halo_copies = []
    for n, (dr, dc) in enumerate(
        (dr, dc) for dr in (-1, 0, 1) for dc in (-1, 0, 1) if (dr, dc) != (0, 0)
    ):
        rows = {-1: (2, 34, 2), 0: (2, 2, 32), 1: (32, 0, 2)}[dr]
        cols = {-1: (1, 9, 1), 0: (1, 1, 8), 1: (8, 0, 1)}[dc]
        halo_copies.append(
            pltpu.make_async_remote_copy(
                src_ref=grid_v.at[pl.ds(rows[0], rows[2]), pl.ds(cols[0], cols[2])],
                dst_ref=grid_v.at[pl.ds(rows[1], rows[2]), pl.ds(cols[1], cols[2])],
                send_sem=halo_send.at[n],
                recv_sem=halo_recv.at[n],
                device_id=((row + dr + 8) % 8, (col + dc + 16) % 16),
                device_id_type=MESH,
            )
        )
        halo_copies[-1].start()

    for copy in route_copies:
        copy.wait()

    table = all_routes[...].T
    keys = subs * 32 + local_of(table)
    hits = owner_of(table) == me
    first = jnp.min(jnp.where(hits, keys, BIG), axis=0, keepdims=True) & 31
    last = jnp.max(jnp.where(hits, keys, 0), axis=0, keepdims=True) & 31
    slots[pl.ds(0, 1), :] = first
    slots[pl.ds(1, 1), :] = last
    to_scalars = pltpu.make_async_copy(slots, slots_smem, local_sem.at[0])
    to_scalars.start()
    to_scalars.wait()

    def fill(target):
        for s in range(2):
            send[2 * target + s] = normed[slots_smem[s, target]]

    data_copies = []

    def launch(n):
        target = peer(OFFSETS[n])
        number = target[0] * 16 + target[1]
        data_copies.append(
            pltpu.make_async_remote_copy(
                src_ref=send.at[pl.ds(2 * number, 2)],
                dst_ref=recv_ref.at[pl.ds(2 * me, 2)],
                send_sem=data_send.at[n],
                recv_sem=data_recv.at[n],
                device_id=target,
                device_id_type=MESH,
            )
        )
        data_copies[-1].start()

    lag = 2
    for n, offset in enumerate(OFFSETS):
        target = peer(offset)
        fill(target[0] * 16 + target[1])
        if n >= lag:
            launch(n - lag)
    for s in range(2):
        recv_ref[2 * me + s] = normed[slots_smem[s, me]]
    for n in range(len(OFFSETS) - lag, len(OFFSETS)):
        launch(n)

    for copy in halo_copies:
        copy.wait()
    keep_top, keep_bottom = row > 0, row < 7
    keep_left, keep_right = col > 0, col < 15

    def widen(block, keep):
        return jnp.where(keep, block.astype(jnp.float32), 0.0)

    @pl.loop(0, 36)
    def _(i):
        inside = jnp.logical_and(
            jnp.logical_or(i >= 2, keep_top), jnp.logical_or(i < 34, keep_bottom)
        )
        for j in range(10):
            keep = inside
            if j == 0:
                keep = jnp.logical_and(inside, keep_left)
            if j == 9:
                keep = jnp.logical_and(inside, keep_right)
            padded[i, pl.ds(8 * j, 8), :] = widen(grid_v[i, j], keep)

    @pl.loop(0, 8)
    def _(j):
        weights = [[lce_ref[a, pl.ds(b, 1), :] for b in range(5)] for a in range(5)]
        for i in range(4):
            totals = [None] * 8
            for line in range(12):
                for b in range(5):
                    window = padded[8 * i + line, pl.ds(8 * j + 6 + b, 8), :]
                    for a in range(5):
                        t = line - a
                        if 0 <= t < 8:
                            term = window * weights[a][b]
                            totals[t] = term if totals[t] is None else totals[t] + term
            for t in range(8):
                ctx_ref[8 * i + j, pl.ds(8 * t, 8), :] = totals[t]

    for copy in data_copies:
        copy.wait()


def exchange(routes, image, gain, qkv, lce):
    vmem = pl.BlockSpec(memory_space=pltpu.VMEM)
    dma = pltpu.SemaphoreType.DMA
    return pl.pallas_call(
        exchange_kernel,
        out_shape=(
            jax.ShapeDtypeStruct((256, 64, 128), jnp.bfloat16),
            jax.ShapeDtypeStruct((32, 64, 128), jnp.bfloat16),
            jax.ShapeDtypeStruct((32, 64, 128), jnp.float32),
            jax.ShapeDtypeStruct((1, 128), jnp.int32),
        ),
        in_specs=[vmem] * 5,
        out_specs=(vmem,) * 4,
        scratch_shapes=[
            pltpu.VMEM((32, 64, 128), jnp.bfloat16),
            pltpu.VMEM((256, 64, 128), jnp.bfloat16),
            pltpu.VMEM((1, 128), jnp.int32),
            pltpu.VMEM((128, 128), jnp.int32),
            pltpu.VMEM((2, 128), jnp.int32),
            pltpu.SMEM((2, 128), jnp.int32),
            pltpu.VMEM((36, 10, 8, 128), jnp.bfloat16),
            pltpu.VMEM((36, 80, 128), jnp.float32),
            dma((127,)), dma((127,)), dma((8,)), dma((8,)), dma((127,)), dma((127,)), dma((1,)),
        ],
        compiler_params=pltpu.CompilerParams(
            collective_id=0, has_side_effects=True, vmem_limit_bytes=40 << 20
        ),
        name="exchange",
    )(routes, image, gain, qkv, lce)


def attend_kernel(
    pos_ref, recv_ref, q_ref, ctx_ref, image_ref, key_ref, value_ref, out_w_ref, gain_ref,
    up_ref, down_ref, out_ref, combined,
):
    factor = 32 ** (-0.5) / math.log(2)
    lane_head = lax.broadcasted_iota(jnp.int32, (64, 128), 1) // 32
    low_lanes = lax.broadcasted_iota(jnp.int32, (32, 128), 1) < 64
    over_last = (((1,), (1,)), ((), ()))

    def attend(r, parity):
        base = (r // 8) * 32 + r % 8
        tokens = jnp.concatenate([recv_ref[pos_ref[0, base + 8 * t]] for t in range(4)], axis=0)
        keys = jnp.dot(tokens, key_ref[...], preferred_element_type=jnp.float32)
        values = lax.dot_general(
            value_ref[...], tokens, over_last, preferred_element_type=jnp.float32
        )
        queries = q_ref[r]
        zero = jnp.zeros_like(queries)
        stacked = jnp.concatenate(
            [jnp.where(lane_head == h, queries, zero) for h in range(HEADS)], axis=0
        )
        scores = lax.dot_general(
            keys.astype(jnp.bfloat16), stacked, over_last, preferred_element_type=jnp.float32
        )
        expons = jnp.exp2((scores - jnp.max(scores, axis=0, keepdims=True)) * factor)
        weights = expons * (1.0 / jnp.sum(expons, axis=0, keepdims=True))
        blended = jnp.dot(
            values.astype(jnp.bfloat16), weights.astype(jnp.bfloat16),
            preferred_element_type=jnp.float32,
        )
        parts = []
        for h in range(HEADS):
            part = blended[32 * h : 32 * h + 32, 128 * (h // 2) : 128 * (h // 2) + 128]
            if h % 2 != parity:
                part = pltpu.roll(part, 64, 1)
            parts.append(part)
        return parts

    @pl.loop(0, 16)
    def _(p):
        even, odd = attend(2 * p, 0), attend(2 * p + 1, 1)
        both = jnp.concatenate([jnp.where(low_lanes, a, b) for a, b in zip(even, odd)], axis=0)
        attended = both.T.reshape(2, 64, 128)
        combined[pl.ds(2 * p, 2)] = (attended + ctx_ref[pl.ds(2 * p, 2)]).astype(jnp.bfloat16)

    @pl.loop(0, 4)
    def _(i):
        strip = to_strip(image_ref[pl.ds(8 * i, 8)].astype(jnp.float32)).reshape(512, 128)
        mixed = jnp.dot(
            combined[pl.ds(8 * i, 8)].reshape(512, 128), out_w_ref[...],
            preferred_element_type=jnp.float32,
        )
        stored = (strip + mixed).astype(jnp.bfloat16).astype(jnp.float32)
        second = layer_norm(stored, gain_ref[...]).astype(jnp.bfloat16)
        lifted = jnp.dot(second, up_ref[...], preferred_element_type=jnp.float32)
        hidden = jax.nn.gelu(lifted, approximate=True).astype(jnp.bfloat16)
        lowered = jnp.dot(hidden, down_ref[...], preferred_element_type=jnp.float32)
        refined = (stored + lowered).reshape(8, 64, 128)
        out_ref[pl.ds(8 * i, 8)] = to_strip(refined).astype(jnp.bfloat16)


def attend(pos, recv, q, ctx, image, key_w, value_w, out_w, gain, up, down):
    vmem = pl.BlockSpec(memory_space=pltpu.VMEM)
    return pl.pallas_call(
        attend_kernel,
        out_shape=jax.ShapeDtypeStruct((32, 64, 128), jnp.bfloat16),
        in_specs=[pl.BlockSpec(memory_space=pltpu.SMEM)] + [vmem] * 10,
        out_specs=vmem,
        scratch_shapes=[pltpu.VMEM((32, 64, 128), jnp.bfloat16)],
        compiler_params=pltpu.CompilerParams(vmem_limit_bytes=40 << 20),
        name="attend",
    )(pos, recv, q, ctx, image, key_w, value_w, out_w, gain, up, down)


def body(
    image, routes, norm_gain, qkv_weight, lce_weight, out_weight, mlp_gain, up_weight, down_weight
):
    recv, q, ctx, pos = exchange(
        routes.transpose(0, 2, 1), image, norm_gain[None], qkv_weight, lce_weight
    )
    return attend(
        pos, recv, q, ctx, image, qkv_weight[:, 128:256], qkv_weight[:, 256:].T, out_weight,
        mlp_gain[None], up_weight, down_weight,
    )


def solution(mesh):
    in_specs = (P("rows", "cols", None), P("rows", "cols", None), P(), P(), P(), P(), P(), P(), P())
    out_specs = P("rows", "cols", None)
    return jax.shard_map(body, mesh=mesh, in_specs=in_specs, out_specs=out_specs, check_vma=False)
```

time: 196 us -> 104 us (0.53)
  Pallas kernels: 0 us -> 95 us
  waiting for transfers between devices: 94.3 us -> 0 us
  starting transfers between devices: 35.3 us -> 0 us
  local copies, waits for them, and re-layouts: 37.6 us -> 8.1 us
  matrix products: 17 us -> 0 us
  other arithmetic: 9.26 us -> 0 us
    pallas_call x0 -> x2, Pallas kernels: none -> 95 us  [the longest x1 71.3 us: exchange(): pl.pallas_call(exchange_kernel, out_shape=(jax.ShapeDtypeStruct((256, 64,...]
    ppermute x4 -> x0, waiting for transfers between devices: 90.1 us -> none  [the longest x2 86.7 us: padded_2(): lax.ppermute(lax.slice_in_dim(block, block.shape[dim] - width, None, axis...]
    ppermute x4 -> x0, starting transfers between devices: 17.7 us -> none  [the longest x2 14.3 us: padded_2(): lax.ppermute(lax.slice_in_dim(block, block.shape[dim] - width, None, axis...]
    all_to_all x2 -> x0, starting transfers between devices: 17.6 us -> none  [one_exchange(): lax.all_to_all(pieces, axis, split_axis=0, concat_axis=0, tiled=True)]
    gather x2 -> x0, local copies, waits for them, and re-layouts: 14.7 us -> none  [the longest x1 8.47 us: body(): keyvals[requested.reshape(-1)]]
    dot_general x7 -> x0, matrix products: 12.8 us -> none  [the longest x1 8.09 us: body(): jnp.dot(combined.reshape(-1, channels), out_weight, preferred_element_typ...]
    dynamic_slice x16 -> x0, local copies, waits for them, and re-layouts: 11.7 us -> none  [body(): lax.map(attend, (queries.reshape(group_count, group_size, region_area, ch...]
    unnamed x75 -> x19, local copies, waits for them, and re-layouts: 0.98 us -> 7.32 us
  transfers between devices with their start and end apart: 6 -> 0, of which waited for: 4 -> 0; matrix products, arithmetic and copies ran while one was open for 5% -> 0% of each run, Pallas kernels for 0% -> 0%
where the time goes in v1:
time: 104 us; the launch traced here: 103 us
  Pallas kernels  95 us (91%)
  local copies, waits for them, and re-layouts  8.1 us (8%)
    pallas_call x1, Pallas kernels, exchange(): pl.pallas_call(exchange_kernel, out_shape=(jax.ShapeDtypeStruct((256, 64,...  71.3 us
    pallas_call x1, Pallas kernels, attend(): pl.pallas_call(attend_kernel, out_shape=jax.ShapeDtypeStruct((32, 64, 128...  23.6 us
    unnamed x19, local copies, waits for them, and re-layouts  7.32 us

profile of v1, /device:TPU:1, one launch (start us, length us, event | category | flops | bytes accessed | tf_op | source)
XLA Modules:
  0.0 103.1 jit_solution(7393036705970163123)
XLA Ops:
  0.0 0.8 fusion
  0.8 0.1 copy.11
  0.9 0.0 copy-start
  0.9 1.0 %copy-done = bf16[32,64,128]{2,1,0:T(8,128)(2,1)S(1)} copy-done((bf16[32,64,128]{2,1,0:T(8,128)(2,1)S(1)}, bf16[32,64,128]{2,1,0:T(8,128)(2,1)}, u32[]{:S(2)}) %copy-start) | copy-done | bytes 524312
  1.9 0.0 copy-start.1
  2.0 0.9 copy-done.1
  2.8 0.0 copy-start.5
  2.8 0.7 copy-done.5
  3.6 0.0 copy-start.6
  3.6 0.7 copy-done.6
  4.3 0.0 copy-start.7
  4.3 0.7 copy-done.7
  4.9 71.3 %exchange.1 = (bf16[256,64,128]{2,1,0:T(8,128)(2,1)S(1)}, bf16[32,64,128]{2,1,0:T(8,128)(2,1)S(1)}, f32[32,64,128]{2,1,0:T(8,128)S(1)}, s32[1,128]{1,0:T(1,128)S(1)}) custom-call(s32[4,4,8]{2,1,0:T(4,128)S(1)} %bitcast.5, bf16[32,64,128]{2,1,0:T(8,128)(2,1)S(1)} %copy-done, f32[1,128]{1,0:T(1,128)S(1)} %bitcast.6, bf16[128,384]{1,0:T(8,128)(2,1)S(1)} %copy-done.1, ...), custom_call_target="tpu_custom_call" | custom-call | tf_op jit(solution)/shard_map/exchange/pallas_call | solution.py:216
  76.3 0.0 copy-start.2
  76.3 0.9 copy-done.2
  77.2 0.0 copy-start.3
  77.2 0.9 copy-done.3
  78.1 0.0 copy-start.4
  78.1 0.8 copy-done.4
  78.8 0.0 copy-start.8
  78.8 0.7 copy-done.8
  79.5 23.6 %attend.1 = bf16[32,64,128]{2,1,0:T(8,128)(2,1)} custom-call(s32[1,128]{1,0:T(1,128)S(1)} %get-tuple-element.9.pos_ref, bf16[256,64,128]{2,1,0:T(8,128)(2,1)S(1)} %get-tuple-element.10.recv_ref, bf16[32,64,128]{2,1,0:T(8,128)(2,1)S(1)} %get-tuple-element.11.q_ref, f32[32,64,128]{2,1,0:T(8,128)S(1)} %get-tuple-element.12.ctx_ref, ...), custom_call_target="tpu_custom_call" | custom-call | tf_op jit(solution)/shard_map/attend/pallas_call | solution.py:307
Async XLA Ops:
  0.9 1.1 %copy-start = (bf16[32,64,128]{2,1,0:T(8,128)(2,1)S(1)}, bf16[32,64,128]{2,1,0:T(8,128)(2,1)}, u32[]{:S(2)}) copy-start(bf16[32,64,128]{2,1,0:T(8,128)(2,1)} %image_ref.3) | copy-start | bytes 1572868
  1.9 0.9 copy-start.1
  2.8 0.7 copy-start.5
  3.6 0.7 copy-start.6
  4.3 0.7 copy-start.7
  76.3 0.9 copy-start.2
  77.2 0.9 copy-start.3
  78.1 0.8 copy-start.4
  78.8 0.7 copy-start.8

commit v2 on v1

v2 whole, which is shorter than its diff:
```python
import functools
import itertools
import math

import jax
import jax.numpy as jnp
from jax import lax
from jax.experimental import pallas as pl
from jax.experimental.pallas import tpu as pltpu
from jax.sharding import PartitionSpec as P

MESH = pl.DeviceIdType.MESH
HEADS = 4
EPSILON = 1e-06
BIG = 1 << 20


def hops(offset):
    return sum(min(step, 4 - step) for step in offset[1:])


OFFSETS = sorted(
    (o for o in itertools.product(range(2), range(4), range(4), range(4)) if any(o)), key=hops
)


def layer_norm(floats, gain):
    centered = floats - jnp.mean(floats, axis=-1, keepdims=True)
    spread = jnp.mean(centered * centered, axis=-1, keepdims=True)
    return centered * lax.rsqrt(spread + EPSILON) * gain


def owner_of(route):
    return ((route >> 9) << 4) | ((route >> 3) & 15)


def local_of(route):
    return (((route >> 7) & 3) << 3) | (route & 7)


def to_strip(blocks):
    return blocks.reshape(8, 8, 8, 128).transpose(1, 0, 2, 3).reshape(8, 64, 128)


def block_kernel(
    image_hbm, routes_hbm, norm_gain_hbm, qkv_hbm, lce_hbm, out_w_hbm, mlp_gain_hbm, up_hbm, down_hbm,
    out_hbm,
    image_ref, routes_ref, norm_gain_ref, qkv_ref, lce_ref, out_w_ref, mlp_gain_ref, up_ref, down_ref,
    normed, send, recv, keys_ref, values_ref, queries_ref, ctx_ref, combined, refined_ref,
    my_routes, all_routes, slots, slots_smem, place, place_smem, grid_v, padded,
    load_sem, route_send, route_recv, halo_send, halo_recv, data_send, data_recv, local_sem, out_sem,
):
    row, col = lax.axis_index("rows"), lax.axis_index("cols")
    chip_y, core = row // 2, row % 2
    chip_z, chip_x = col // 4, col % 4
    me = row * 16 + col
    over_last = (((1,), (1,)), ((), ()))
    over_first = (((0,), (0,)), ((), ()))

    def peer(offset):
        dc, dy, dz, dx = offset
        return (
            (chip_y + dy) % 4 * 2 + (core + dc) % 2,
            (chip_z + dz) % 4 * 4 + (chip_x + dx) % 4,
        )

    pairs = [
        (image_hbm, image_ref), (routes_hbm, routes_ref), (qkv_hbm, qkv_ref),
        (norm_gain_hbm, norm_gain_ref), (lce_hbm, lce_ref), (out_w_hbm, out_w_ref),
        (mlp_gain_hbm, mlp_gain_ref), (up_hbm, up_ref), (down_hbm, down_ref),
    ]
    loads = [pltpu.make_async_copy(a, b, load_sem.at[n]) for n, (a, b) in enumerate(pairs)]
    for load in loads:
        load.start()
    barrier = pltpu.get_barrier_semaphore()
    for offset in reversed(OFFSETS):
        pl.semaphore_signal(barrier, inc=1, device_id=peer(offset), device_id_type=MESH)
    for load in loads:
        load.wait()

    mine = jnp.concatenate(
        [routes_ref[i, t : t + 1, :] for i in range(4) for t in range(4)], axis=1
    )
    my_routes[...] = mine
    all_routes[pl.ds(me, 1), :] = mine

    gain = norm_gain_ref[...]
    for i in range(4):
        strip = image_ref[pl.ds(8 * i, 8)].astype(jnp.float32)
        strip = to_strip(layer_norm(strip, gain)).astype(jnp.bfloat16)
        normed[pl.ds(8 * i, 8)] = strip
        values = jnp.dot(
            strip.reshape(512, 128), qkv_ref[:, 256:384], preferred_element_type=jnp.float32
        )
        values = values.reshape(8, 8, 8, 128).transpose(1, 0, 2, 3)
        grid_v[pl.ds(2 + 8 * i, 8), pl.ds(1, 8)] = values.astype(jnp.bfloat16)

    lanes = lax.broadcasted_iota(jnp.int32, (128, 128), 1)
    subs = lax.broadcasted_iota(jnp.int32, (128, 128), 0)
    owners = jnp.broadcast_to(owner_of(mine), (128, 128))
    same = jnp.logical_and(owners == owners.T, subs < lanes)
    second = jnp.max(jnp.where(same, 1, 0), axis=0, keepdims=True)
    place[...] = owner_of(mine) * 2 + second
    to_places = pltpu.make_async_copy(place, place_smem, local_sem.at[1])
    to_places.start()

    pl.semaphore_wait(barrier, len(OFFSETS))

    route_copies = []
    for n, offset in enumerate(OFFSETS[::-1]):
        route_copies.append(
            pltpu.make_async_remote_copy(
                src_ref=my_routes,
                dst_ref=all_routes.at[pl.ds(me, 1)],
                send_sem=route_send.at[n],
                recv_sem=route_recv.at[n],
                device_id=peer(offset),
                device_id_type=MESH,
            )
        )
        route_copies[-1].start()

    halo_copies = []
    for n, (dr, dc) in enumerate(
        (dr, dc) for dr in (-1, 0, 1) for dc in (-1, 0, 1) if (dr, dc) != (0, 0)
    ):
        rows = {-1: (2, 34, 2), 0: (2, 2, 32), 1: (32, 0, 2)}[dr]
        cols = {-1: (1, 9, 1), 0: (1, 1, 8), 1: (8, 0, 1)}[dc]
        halo_copies.append(
            pltpu.make_async_remote_copy(
                src_ref=grid_v.at[pl.ds(rows[0], rows[2]), pl.ds(cols[0], cols[2])],
                dst_ref=grid_v.at[pl.ds(rows[1], rows[2]), pl.ds(cols[1], cols[2])],
                send_sem=halo_send.at[n],
                recv_sem=halo_recv.at[n],
                device_id=((row + dr + 8) % 8, (col + dc + 16) % 16),
                device_id_type=MESH,
            )
        )
        halo_copies[-1].start()

    for copy in route_copies:
        copy.wait()

    table = all_routes[...].T
    order = subs * 32 + local_of(table)
    hits = owner_of(table) == me
    first = jnp.min(jnp.where(hits, order, BIG), axis=0, keepdims=True) & 31
    last = jnp.max(jnp.where(hits, order, 0), axis=0, keepdims=True) & 31
    slots[pl.ds(0, 1), :] = first
    slots[pl.ds(1, 1), :] = last
    to_scalars = pltpu.make_async_copy(slots, slots_smem, local_sem.at[0])
    to_scalars.start()
    to_scalars.wait()

    def fill(target):
        for s in range(2):
            send[2 * target + s] = normed[slots_smem[s, target]]

    data_copies = []

    def launch(n):
        target = peer(OFFSETS[n])
        number = target[0] * 16 + target[1]
        data_copies.append(
            pltpu.make_async_remote_copy(
                src_ref=send.at[pl.ds(2 * number, 2)],
                dst_ref=recv.at[pl.ds(2 * me, 2)],
                send_sem=data_send.at[n],
                recv_sem=data_recv.at[n],
                device_id=target,
                device_id_type=MESH,
            )
        )
        data_copies[-1].start()

    lag = 2
    for n, offset in enumerate(OFFSETS):
        target = peer(offset)
        fill(target[0] * 16 + target[1])
        if n >= lag:
            launch(n - lag)
    for s in range(2):
        recv[2 * me + s] = normed[slots_smem[s, me]]
    for n in range(len(OFFSETS) - lag, len(OFFSETS)):
        launch(n)

    query_w = qkv_ref[:, 0:128].T
    feature_head = lax.broadcasted_iota(jnp.int32, (128, 256), 0) // 32
    across_head = lax.broadcasted_iota(jnp.int32, (128, 256), 1) // 64
    own_head = feature_head == across_head

    @pl.loop(0, 32)
    def _(r):
        tokens = normed[r]
        wide = lax.dot_general(
            query_w, jnp.concatenate([tokens] * 4, axis=0), over_last,
            preferred_element_type=jnp.float32,
        )
        queries_ref[r] = jnp.where(own_head, wide, 0.0).astype(jnp.bfloat16)

    for copy in halo_copies:
        copy.wait()
    keep_top, keep_bottom = row > 0, row < 7
    keep_left, keep_right = col > 0, col < 15

    @pl.loop(0, 36)
    def _(i):
        inside = jnp.logical_and(
            jnp.logical_or(i >= 2, keep_top), jnp.logical_or(i < 34, keep_bottom)
        )
        for j in range(10):
            keep = inside
            if j == 0:
                keep = jnp.logical_and(inside, keep_left)
            if j == 9:
                keep = jnp.logical_and(inside, keep_right)
            padded[i, pl.ds(8 * j, 8), :] = jnp.where(keep, grid_v[i, j].astype(jnp.float32), 0.0)

    @pl.loop(0, 8)
    def _(j):
        weights = [[lce_ref[a, pl.ds(b, 1), :] for b in range(5)] for a in range(5)]
        for i in range(4):
            totals = [None] * 8
            for line in range(12):
                for b in range(5):
                    window = padded[8 * i + line, pl.ds(8 * j + 6 + b, 8), :]
                    for a in range(5):
                        t = line - a
                        if 0 <= t < 8:
                            term = window * weights[a][b]
                            totals[t] = term if totals[t] is None else totals[t] + term
            for t in range(8):
                ctx_ref[8 * i + j, pl.ds(8 * t, 8), :] = totals[t]

    def project(source):
        tokens = recv[pl.ds(2 * source, 2)].reshape(128, 128)
        both = jnp.dot(tokens, qkv_ref[:, 128:384], preferred_element_type=jnp.float32)
        both = both.astype(jnp.bfloat16)
        keys_ref[pl.ds(2 * source, 2)] = both[:, :128].reshape(2, 64, 128)
        values_ref[pl.ds(2 * source, 2)] = both[:, 128:].reshape(2, 64, 128)

    project(me)
    for n, offset in enumerate(OFFSETS):
        dc, dy, dz, dx = offset
        source = peer((dc, 4 - dy, 4 - dz, 4 - dx))
        data_copies[n].wait_recv()
        project(source[0] * 16 + source[1])
    to_places.wait()

    factor = 32 ** (-0.5) / math.log(2)
    low_lanes = lax.broadcasted_iota(jnp.int32, (32, 128), 1) < 64

    def attend(r, parity):
        base = (r // 8) * 32 + r % 8
        spots = [place_smem[0, base + 8 * t] for t in range(4)]
        keys = jnp.concatenate([keys_ref[s] for s in spots], axis=0)
        values = jnp.concatenate([values_ref[s] for s in spots], axis=0)
        scores = jnp.dot(keys, queries_ref[r], preferred_element_type=jnp.float32)
        expons = jnp.exp2((scores - jnp.max(scores, axis=0, keepdims=True)) * factor)
        weights = expons * (1.0 / jnp.sum(expons, axis=0, keepdims=True))
        blended = lax.dot_general(
            values, weights.astype(jnp.bfloat16), over_first, preferred_element_type=jnp.float32
        )
        parts = []
        for h in range(HEADS):
            part = blended[32 * h : 32 * h + 32, 128 * (h // 2) : 128 * (h // 2) + 128]
            if h % 2 != parity:
                part = pltpu.roll(part, 64, 1)
            parts.append(part)
        return parts

    @pl.loop(0, 32 // GROUP)
    def _(g):
        for p in range(GROUP // 2):
            r = g * GROUP + 2 * p
            even, odd = attend(r, 0), attend(r + 1, 1)
            both = jnp.concatenate([jnp.where(low_lanes, a, b) for a, b in zip(even, odd)], axis=0)
            attended = both.T.reshape(2, 64, 128)
            combined[pl.ds(r, 2)] = (attended + ctx_ref[pl.ds(r, 2)]).astype(jnp.bfloat16)

    @pl.loop(0, 4)
    def _(i):
        strip = to_strip(image_ref[pl.ds(8 * i, 8)].astype(jnp.float32)).reshape(512, 128)
        mixed = jnp.dot(
            combined[pl.ds(8 * i, 8)].reshape(512, 128), out_w_ref[...],
            preferred_element_type=jnp.float32,
        )
        stored = (strip + mixed).astype(jnp.bfloat16).astype(jnp.float32)
        second = layer_norm(stored, mlp_gain_ref[...]).astype(jnp.bfloat16)
        lifted = jnp.dot(second, up_ref[...], preferred_element_type=jnp.float32)
        hidden = jax.nn.gelu(lifted, approximate=True).astype(jnp.bfloat16)
        lowered = jnp.dot(hidden, down_ref[...], preferred_element_type=jnp.float32)
        refined = (stored + lowered).reshape(8, 64, 128)
        refined_ref[pl.ds(8 * i, 8)] = to_strip(refined).astype(jnp.bfloat16)

    store = pltpu.make_async_copy(refined_ref, out_hbm, out_sem)
    store.start()
    for copy in data_copies:
        copy.wait_send()
    store.wait()


GROUP = 4


def body(
    image, routes, norm_gain, qkv_weight, lce_weight, out_weight, mlp_gain, up_weight, down_weight
):
    operands = (
        image, routes.transpose(0, 2, 1), norm_gain[None], qkv_weight, lce_weight, out_weight,
        mlp_gain[None], up_weight, down_weight,
    )
    hbm = pl.BlockSpec(memory_space=pl.ANY)
    dma = pltpu.SemaphoreType.DMA
    bf16, f32, i32 = jnp.bfloat16, jnp.float32, jnp.int32
    return pl.pallas_call(
        block_kernel,
        out_shape=jax.ShapeDtypeStruct((32, 64, 128), bf16),
        in_specs=[hbm] * 9,
        out_specs=hbm,
        scratch_shapes=[pltpu.VMEM(x.shape, x.dtype) for x in operands] + [
            pltpu.VMEM((32, 64, 128), bf16),
            pltpu.VMEM((256, 64, 128), bf16),
            pltpu.VMEM((256, 64, 128), bf16),
            pltpu.VMEM((256, 64, 128), bf16),
            pltpu.VMEM((256, 64, 128), bf16),
            pltpu.VMEM((32, 128, 256), bf16),
            pltpu.VMEM((32, 64, 128), f32),
            pltpu.VMEM((32, 64, 128), bf16),
            pltpu.VMEM((32, 64, 128), bf16),
            pltpu.VMEM((1, 128), i32),
            pltpu.VMEM((128, 128), i32),
            pltpu.VMEM((2, 128), i32),
            pltpu.SMEM((2, 128), i32),
            pltpu.VMEM((1, 128), i32),
            pltpu.SMEM((1, 128), i32),
            pltpu.VMEM((36, 10, 8, 128), bf16),
            pltpu.VMEM((36, 80, 128), f32),
            dma((9,)), dma((127,)), dma((127,)), dma((8,)), dma((8,)), dma((127,)), dma((127,)),
            dma((2,)), dma(()),
        ],
        compiler_params=pltpu.CompilerParams(
            collective_id=0, has_side_effects=True, vmem_limit_bytes=60 << 20
        ),
        name="block",
    )(*operands)


def solution(mesh):
    in_specs = (P("rows", "cols", None), P("rows", "cols", None), P(), P(), P(), P(), P(), P(), P())
    out_specs = P("rows", "cols", None)
    return jax.shard_map(body, mesh=mesh, in_specs=in_specs, out_specs=out_specs, check_vma=False)
```

time: 104 us -> 90.7 us (0.87)
  Pallas kernels: 95 us -> 88.7 us
  local copies, waits for them, and re-layouts: 8.1 us -> 1.87 us
    pallas_call x2 -> x1, Pallas kernels: 95 us -> 88.7 us  [body(): pl.pallas_call(block_kernel, out_shape=jax.ShapeDtypeStruct((32, 64, 128)...]
    unnamed x19 -> x1, local copies, waits for them, and re-layouts: 7.32 us -> 1.87 us
where the time goes in v2:
time: 90.7 us; the launch traced here: 90.5 us
  Pallas kernels  88.7 us (98%)
  local copies, waits for them, and re-layouts  1.87 us (2%)
    pallas_call x1, Pallas kernels, body(): pl.pallas_call(block_kernel, out_shape=jax.ShapeDtypeStruct((32, 64, 128)...  88.7 us
    unnamed x1, local copies, waits for them, and re-layouts  1.87 us

profile of v2, /device:TPU:1, one launch (start us, length us, event | category | flops | bytes accessed | tf_op | source)
XLA Modules:
  0.0 90.5 jit_solution(13943886864640624966)
XLA Ops:
  0.0 88.7 %block.1 = bf16[32,64,128]{2,1,0:T(8,128)(2,1)} custom-call(bf16[32,64,128]{2,1,0:T(8,128)(2,1)} %image_hbm.1, s32[4,4,8]{2,1,0:T(4,128)} %bitcast.3, f32[1,128]{1,0:T(1,128)} %bitcast.4, bf16[128,384]{1,0:T(8,128)(2,1)} %qkv_hbm.1, f32[5,5,128]{2,1,0:T(8,128)} %lce_hbm.1, bf16[128,128]{1,0:T(8,128)(2,1)} %out_w_hbm.1, f32[1,128]{1,0:T(1,128)} %bitcast.5, ...), custom_call_target="tpu_custom_call" | custom-call | tf_op jit(solution)/shard_map/block/pallas_call | solution.py:316
  88.7 1.9 %copy.11 = bf16[32,64,128]{2,1,0:T(8,128)(2,1)} copy(bf16[32,64,128]{2,1,0:T(8,128)(2,1)} %block.1) | data formatting | bytes 1048576

commit v3 on v2

--- a/solution.py
+++ b/solution.py
@@ -24,6 +24,19 @@
 )
 
 
+PART = 16
+PLANE = sorted(
+    (o for o in itertools.product(range(2), range(4), range(4)) if any(o)), key=hops
+)
+BATCHES = (range(0, 8), range(8, 16), range(16, 22), range(22, 27), range(27, 31))
+BATCH_OF = [b for b, members in enumerate(BATCHES) for _ in members]
+
+
+def widened(part, offset):
+    dc, first, second = offset
+    return ((dc, first, second, 0), (dc, 0, second, first), (dc, first, 0, second))[part]
+
+
 def layer_norm(floats, gain):
     centered = floats - jnp.mean(floats, axis=-1, keepdims=True)
     spread = jnp.mean(centered * centered, axis=-1, keepdims=True)
@@ -44,16 +57,22 @@
 
 def block_kernel(
     image_hbm, routes_hbm, norm_gain_hbm, qkv_hbm, lce_hbm, out_w_hbm, mlp_gain_hbm, up_hbm, down_hbm,
-    out_hbm,
+    refined_ref,
     image_ref, routes_ref, norm_gain_ref, qkv_ref, lce_ref, out_w_ref, mlp_gain_ref, up_ref, down_ref,
-    normed, send, recv, keys_ref, values_ref, queries_ref, ctx_ref, combined, refined_ref,
+    lines, straight, send, recv, keys_ref, values_ref, queries_ref, ctx_ref, combined,
     my_routes, all_routes, slots, slots_smem, place, place_smem, grid_v, padded,
-    load_sem, route_send, route_recv, halo_send, halo_recv, data_send, data_recv, local_sem, out_sem,
+    load_sem, send_sem, recv_sem, local_sem,
 ):
     row, col = lax.axis_index("rows"), lax.axis_index("cols")
     chip_y, core = row // 2, row % 2
     chip_z, chip_x = col // 4, col % 4
     me = row * 16 + col
+    spots = (chip_x, chip_y, chip_z)
+    relays = (
+        (core * 4 + chip_z) * 4 + chip_y,
+        (core * 4 + chip_z) * 4 + chip_x,
+        (core * 4 + chip_y) * 4 + chip_x,
+    )
     over_last = (((1,), (1,)), ((), ()))
     over_first = (((0,), (0,)), ((), ()))
 
@@ -88,7 +107,9 @@
     for i in range(4):
         strip = image_ref[pl.ds(8 * i, 8)].astype(jnp.float32)
         strip = to_strip(layer_norm(strip, gain)).astype(jnp.bfloat16)
-        normed[pl.ds(8 * i, 8)] = strip
+        for p in range(3):
+            lines[p][spots[p], pl.ds(8 * i, 8)] = strip[:, PART * p : PART * p + PART]
+        straight[pl.ds(8 * i, 8)] = strip[:, PART * 3 :]
         values = jnp.dot(
             strip.reshape(512, 128), qkv_ref[:, 256:384], preferred_element_type=jnp.float32
         )
@@ -100,7 +121,12 @@
     owners = jnp.broadcast_to(owner_of(mine), (128, 128))
     same = jnp.logical_and(owners == owners.T, subs < lanes)
     second = jnp.max(jnp.where(same, 1, 0), axis=0, keepdims=True)
-    place[...] = owner_of(mine) * 2 + second
+    own = owner_of(mine)
+    oy, oc, oz, ox = own >> 5, (own >> 4) & 1, (own >> 2) & 3, own & 3
+    place[pl.ds(0, 1), :] = ((oc * 4 + oz) * 4 + oy) * 8 + ox * 2 + second
+    place[pl.ds(1, 1), :] = ((oc * 4 + oz) * 4 + ox) * 8 + oy * 2 + second
+    place[pl.ds(2, 1), :] = ((oc * 4 + oy) * 4 + ox) * 8 + oz * 2 + second
+    place[pl.ds(3, 1), :] = own * 2 + second
     to_places = pltpu.make_async_copy(place, place_smem, local_sem.at[1])
     to_places.start()
 
@@ -112,8 +138,8 @@
             pltpu.make_async_remote_copy(
                 src_ref=my_routes,
                 dst_ref=all_routes.at[pl.ds(me, 1)],
-                send_sem=route_send.at[n],
-                recv_sem=route_recv.at[n],
+                send_sem=send_sem.at[0],
+                recv_sem=recv_sem.at[0],
                 device_id=peer(offset),
                 device_id_type=MESH,
             )
@@ -130,76 +156,130 @@
             pltpu.make_async_remote_copy(
                 src_ref=grid_v.at[pl.ds(rows[0], rows[2]), pl.ds(cols[0], cols[2])],
                 dst_ref=grid_v.at[pl.ds(rows[1], rows[2]), pl.ds(cols[1], cols[2])],
-                send_sem=halo_send.at[n],
-                recv_sem=halo_recv.at[n],
+                send_sem=send_sem.at[1],
+                recv_sem=recv_sem.at[1 + n],
                 device_id=((row + dr + 8) % 8, (col + dc + 16) % 16),
                 device_id_type=MESH,
             )
         )
         halo_copies[-1].start()
 
-    for copy in route_copies:
-        copy.wait()
-
-    table = all_routes[...].T
-    order = subs * 32 + local_of(table)
-    hits = owner_of(table) == me
-    first = jnp.min(jnp.where(hits, order, BIG), axis=0, keepdims=True) & 31
-    last = jnp.max(jnp.where(hits, order, 0), axis=0, keepdims=True) & 31
-    slots[pl.ds(0, 1), :] = first
-    slots[pl.ds(1, 1), :] = last
-    to_scalars = pltpu.make_async_copy(slots, slots_smem, local_sem.at[0])
-    to_scalars.start()
-    to_scalars.wait()
-
-    def fill(target):
-        for s in range(2):
-            send[2 * target + s] = normed[slots_smem[s, target]]
-
-    data_copies = []
-
-    def launch(n):
-        target = peer(OFFSETS[n])
-        number = target[0] * 16 + target[1]
-        data_copies.append(
-            pltpu.make_async_remote_copy(
-                src_ref=send.at[pl.ds(2 * number, 2)],
-                dst_ref=recv.at[pl.ds(2 * me, 2)],
-                send_sem=data_send.at[n],
-                recv_sem=data_recv.at[n],
-                device_id=target,
-                device_id_type=MESH,
+    line_copies = []
+    for p in range(3):
+        for step in (1, 3, 2):
+            offset = tuple(step if axis == 3 - (0, 2, 1)[p] else 0 for axis in range(4))
+            line_copies.append(
+                pltpu.make_async_remote_copy(
+                    src_ref=lines[p].at[spots[p]],
+                    dst_ref=lines[p].at[spots[p]],
+                    send_sem=send_sem.at[2 + p],
+                    recv_sem=recv_sem.at[9 + p],
+                    device_id=peer(offset),
+                    device_id_type=MESH,
+                )
             )
-        )
-        data_copies[-1].start()
-
-    lag = 2
-    for n, offset in enumerate(OFFSETS):
-        target = peer(offset)
-        fill(target[0] * 16 + target[1])
-        if n >= lag:
-            launch(n - lag)
-    for s in range(2):
-        recv[2 * me + s] = normed[slots_smem[s, me]]
-    for n in range(len(OFFSETS) - lag, len(OFFSETS)):
-        launch(n)
+            line_copies[-1].start()
 
     query_w = qkv_ref[:, 0:128].T
     feature_head = lax.broadcasted_iota(jnp.int32, (128, 256), 0) // 32
     across_head = lax.broadcasted_iota(jnp.int32, (128, 256), 1) // 64
     own_head = feature_head == across_head
 
-    @pl.loop(0, 32)
-    def _(r):
-        tokens = normed[r]
+    def lay_out(r):
+        tokens = jnp.concatenate(
+            [lines[p][spots[p], r] for p in range(3)] + [straight[r]], axis=0
+        )
         wide = lax.dot_general(
             query_w, jnp.concatenate([tokens] * 4, axis=0), over_last,
             preferred_element_type=jnp.float32,
         )
         queries_ref[r] = jnp.where(own_head, wide, 0.0).astype(jnp.bfloat16)
 
+    @pl.loop(0, 8)
+    def _(i):
+        for j in range(4):
+            lay_out(4 * i + j)
+
+    def wait_bytes(ref, sem):
+        pltpu.make_async_copy(ref, ref, sem).wait()
+
+    wait_bytes(all_routes.at[pl.ds(0, 127)], recv_sem.at[0])
+
+    table = all_routes[...].T
+    order = subs * 32 + local_of(table)
+    table_owner = owner_of(table)
+    for p in range(3):
+        for i in range(4):
+            owner = (
+                row * 16 + chip_z * 4 + i,
+                (i * 2 + core) * 16 + col,
+                row * 16 + i * 4 + chip_x,
+            )[p]
+            hits = table_owner == owner
+            first = jnp.min(jnp.where(hits, order, BIG), axis=0, keepdims=True) & 31
+            last = jnp.max(jnp.where(hits, order, 0), axis=0, keepdims=True) & 31
+            slots[pl.ds(8 * p + 2 * i, 1), :] = first
+            slots[pl.ds(8 * p + 2 * i + 1, 1), :] = last
+    to_scalars = pltpu.make_async_copy(slots, slots_smem, local_sem.at[0])
+    to_scalars.start()
+    to_scalars.wait()
+
+    def fill(p, number, into, base):
+        for i in range(4):
+            for t in range(2):
+                into[base + 2 * i + t] = lines[p][i, slots_smem[8 * p + 2 * i + t, number]]
+
+    def launch(p, n):
+        pltpu.make_async_remote_copy(
+            src_ref=send[p].at[pl.ds(8 * n, 8)],
+            dst_ref=recv[p].at[pl.ds(8 * relays[p], 8)],
+            send_sem=send_sem.at[5 + p],
+            recv_sem=recv_sem.at[12 + len(BATCHES) * p + BATCH_OF[n]],
+            device_id=peer(widened(p, PLANE[n])),
+            device_id_type=MESH,
+        ).start()
+
+    def fill_straight(number, into, base):
+        for t in range(2):
+            into[base + t] = straight[slots_smem[2 * chip_x + t, number]]
+
+    def launch_straight(n):
+        pltpu.make_async_remote_copy(
+            src_ref=send[3].at[pl.ds(2 * n, 2)],
+            dst_ref=recv[3].at[pl.ds(2 * me, 2)],
+            send_sem=send_sem.at[8],
+            recv_sem=recv_sem.at[12 + 3 * len(BATCHES)],
+            device_id=peer(OFFSETS[n]),
+            device_id_type=MESH,
+        ).start()
+
+    pending = []
+
+    def queue(start, *which):
+        pending.append((start, which))
+        if len(pending) > 2:
+            begin, what = pending.pop(0)
+            begin(*what)
+
+    for n, offset in enumerate(OFFSETS):
+        target = peer(offset)
+        fill_straight(target[0] * 16 + target[1], send[3], 2 * n)
+        queue(launch_straight, n)
+    for p in range(3):
+        wait_bytes(lines[p].at[pl.ds(0, 3)], recv_sem.at[9 + p])
+    for n in range(31):
+        for p in range(3):
+            target = peer(widened(p, PLANE[n]))
+            fill(p, target[0] * 16 + target[1], send[p], 8 * n)
+            queue(launch, p, n)
+    for p in range(3):
+        fill(p, me, recv[p], 8 * relays[p])
+    fill_straight(me, recv[3], 2 * me)
+    for begin, what in pending:
+        begin(*what)
+
     for copy in halo_copies:
-        copy.wait()
+        copy.wait_recv()
     keep_top, keep_bottom = row > 0, row < 7
     keep_left, keep_right = col > 0, col < 15
 
@@ -232,19 +312,34 @@
             for t in range(8):
                 ctx_ref[8 * i + j, pl.ds(8 * t, 8), :] = totals[t]
 
-    def project(source):
-        tokens = recv[pl.ds(2 * source, 2)].reshape(128, 128)
+    def project(p, first, count):
+        tokens = recv[p][pl.ds(first, count)].reshape(count * PART, 128)
         both = jnp.dot(tokens, qkv_ref[:, 128:384], preferred_element_type=jnp.float32)
         both = both.astype(jnp.bfloat16)
-        keys_ref[pl.ds(2 * source, 2)] = both[:, :128].reshape(2, 64, 128)
-        values_ref[pl.ds(2 * source, 2)] = both[:, 128:].reshape(2, 64, 128)
-
-    project(me)
-    for n, offset in enumerate(OFFSETS):
-        dc, dy, dz, dx = offset
-        source = peer((dc, 4 - dy, 4 - dz, 4 - dx))
-        data_copies[n].wait_recv()
-        project(source[0] * 16 + source[1])
+        keys_ref[p][pl.ds(first, count)] = both[:, :128].reshape(count, PART, 128)
+        values_ref[p][pl.ds(first, count)] = both[:, 128:].reshape(count, PART, 128)
+
+    for p in range(3):
+        project(p, 8 * relays[p], 8)
+    wait_bytes(recv[3].at[pl.ds(0, 254)], recv_sem.at[12 + 3 * len(BATCHES)])
+
+    @pl.loop(0, 16)
+    def _(i):
+        project(3, 16 * i, 16)
+
+    for batch, p in itertools.product(range(len(BATCHES)), range(3)):
+        members = BATCHES[batch]
+        wait_bytes(
+            recv[p].at[pl.ds(0, 8 * len(members))], recv_sem.at[12 + len(BATCHES) * p + batch]
+        )
+        for n in members:
+            dc, first, second = PLANE[n]
+            y, x, z = chip_y + 4, chip_x + 4, chip_z + 4
+            low, high = ((y, z), (x, z), (x, y))[p]
+            if p == 2:
+                first, second = second, first
+            relay = ((core + dc) % 2 * 4 + (high - second) % 4) * 4 + (low - first) % 4
+            project(p, 8 * relay, 8)
     to_places.wait()
 
     factor = 32 ** (-0.5) / math.log(2)
@@ -252,9 +347,9 @@
 
     def attend(r, parity):
         base = (r // 8) * 32 + r % 8
-        spots = [place_smem[0, base + 8 * t] for t in range(4)]
-        keys = jnp.concatenate([keys_ref[s] for s in spots], axis=0)
-        values = jnp.concatenate([values_ref[s] for s in spots], axis=0)
+        found = [(p, place_smem[p, base + 8 * t]) for t in range(4) for p in range(4)]
+        keys = jnp.concatenate([keys_ref[p][s] for p, s in found], axis=0)
+        values = jnp.concatenate([values_ref[p][s] for p, s in found], axis=0)
         scores = jnp.dot(keys, queries_ref[r], preferred_element_type=jnp.float32)
         expons = jnp.exp2((scores - jnp.max(scores, axis=0, keepdims=True)) * factor)
         weights = expons * (1.0 / jnp.sum(expons, axis=0, keepdims=True))
@@ -293,14 +388,16 @@
         refined = (stored + lowered).reshape(8, 64, 128)
         refined_ref[pl.ds(8 * i, 8)] = to_strip(refined).astype(jnp.bfloat16)
 
-    store = pltpu.make_async_copy(refined_ref, out_hbm, out_sem)
-    store.start()
-    for copy in data_copies:
-        copy.wait_send()
-    store.wait()
-
-
-GROUP = 4
+    wait_bytes(all_routes.at[pl.ds(0, 127)], send_sem.at[0])
+    for copy in halo_copies:
+        wait_bytes(copy.src_ref, send_sem.at[1])
+    for p in range(3):
+        wait_bytes(lines[p].at[pl.ds(0, 3)], send_sem.at[2 + p])
+        wait_bytes(send[p], send_sem.at[5 + p])
+    wait_bytes(send[3], send_sem.at[8])
+
+
+GROUP = 8
 
 
 def body(
@@ -310,40 +407,39 @@
         image, routes.transpose(0, 2, 1), norm_gain[None], qkv_weight, lce_weight, out_weight,
         mlp_gain[None], up_weight, down_weight,
     )
-    hbm = pl.BlockSpec(memory_space=pl.ANY)
+    hbm = pl.BlockSpec(memory_space=pltpu.HBM)
     dma = pltpu.SemaphoreType.DMA
     bf16, f32, i32 = jnp.bfloat16, jnp.float32, jnp.int32
     return pl.pallas_call(
         block_kernel,
         out_shape=jax.ShapeDtypeStruct((32, 64, 128), bf16),
         in_specs=[hbm] * 9,
-        out_specs=hbm,
+        out_specs=pl.BlockSpec(memory_space=pltpu.VMEM),
         scratch_shapes=[pltpu.VMEM(x.shape, x.dtype) for x in operands] + [
-            pltpu.VMEM((32, 64, 128), bf16),
-            pltpu.VMEM((256, 64, 128), bf16),
-            pltpu.VMEM((256, 64, 128), bf16),
-            pltpu.VMEM((256, 64, 128), bf16),
-            pltpu.VMEM((256, 64, 128), bf16),
+            [pltpu.VMEM((4, 32, PART, 128), bf16)] * 3,
+            pltpu.VMEM((32, PART, 128), bf16),
+            [pltpu.VMEM((count, PART, 128), bf16) for count in (248, 248, 248, 254)],
+            [pltpu.VMEM((256, PART, 128), bf16)] * 4,
+            [pltpu.VMEM((256, PART, 128), bf16)] * 4,
+            [pltpu.VMEM((256, PART, 128), bf16)] * 4,
             pltpu.VMEM((32, 128, 256), bf16),
             pltpu.VMEM((32, 64, 128), f32),
             pltpu.VMEM((32, 64, 128), bf16),
-            pltpu.VMEM((32, 64, 128), bf16),
             pltpu.VMEM((1, 128), i32),
             pltpu.VMEM((128, 128), i32),
-            pltpu.VMEM((2, 128), i32),
-            pltpu.SMEM((2, 128), i32),
-            pltpu.VMEM((1, 128), i32),
-            pltpu.SMEM((1, 128), i32),
+            pltpu.VMEM((24, 128), i32),
+            pltpu.SMEM((24, 128), i32),
+            pltpu.VMEM((4, 128), i32),
+            pltpu.SMEM((4, 128), i32),
             pltpu.VMEM((36, 10, 8, 128), bf16),
             pltpu.VMEM((36, 80, 128), f32),
-            dma((9,)), dma((127,)), dma((127,)), dma((8,)), dma((8,)), dma((127,)), dma((127,)),
-            dma((2,)), dma(()),
+            dma((9,)), dma((9,)), dma((13 + 3 * len(BATCHES),)), dma((2,)),
         ],
         compiler_params=pltpu.CompilerParams(
-            collective_id=0, has_side_effects=True, vmem_limit_bytes=60 << 20
+            collective_id=0, has_side_effects=True, vmem_limit_bytes=48 << 20
         ),
         name="block",
-    )(*operands)
+    )(*[pltpu.with_memory_space_constraint(x, pltpu.HBM) for x in operands])
 
 
 def solution(mesh):

time: 90.7 us -> 74.3 us (0.82)
  Pallas kernels: 88.7 us -> 73.4 us
  local copies, waits for them, and re-layouts: 1.87 us -> 0.8 us
    pallas_call x1, Pallas kernels: 88.7 us -> 73.4 us  [body(): pl.pallas_call(block_kernel, out_shape=jax.ShapeDtypeStruct((32, 64, 128)...]
    unnamed x1, local copies, waits for them, and re-layouts: 1.87 us -> 0.8 us
where the time goes in v3:
time: 74.3 us; the launch traced here: 74.2 us
  Pallas kernels  73.4 us (99%)
  local copies, waits for them, and re-layouts  0.8 us (1%)
    pallas_call x1, Pallas kernels, body(): pl.pallas_call(block_kernel, out_shape=jax.ShapeDtypeStruct((32, 64, 128)...  73.4 us

profile of v3, /device:TPU:1, one launch (start us, length us, event | category | flops | bytes accessed | tf_op | source)
XLA Modules:
  0.0 74.2 jit_solution(12070805842404561203)
XLA Ops:
  0.0 73.4 %block.1 = bf16[32,64,128]{2,1,0:T(8,128)(2,1)S(1)} custom-call(bf16[32,64,128]{2,1,0:T(8,128)(2,1)} %image_hbm.1, s32[4,4,8]{2,1,0:T(4,128)} %bitcast.3, f32[1,128]{1,0:T(1,128)} %bitcast.4, bf16[128,384]{1,0:T(8,128)(2,1)} %qkv_hbm.1, f32[5,5,128]{2,1,0:T(8,128)} %lce_hbm.1, bf16[128,128]{1,0:T(8,128)(2,1)} %out_w_hbm.1, f32[1,128]{1,0:T(1,128)} %bitcast.5, ...), custom_call_target="tpu_custom_call" | custom-call | tf_op jit(solution)/shard_map/block/pallas_call | solution.py:413
  73.4 0.8 %copy.11 = bf16[32,64,128]{2,1,0:T(8,128)(2,1)} copy(bf16[32,64,128]{2,1,0:T(8,128)(2,1)S(1)} %block.1) | data formatting | bytes 1048576

commit v4 on v3

--- a/solution.py
+++ b/solution.py
@@ -60,6 +60,7 @@
     refined_ref,
     image_ref, routes_ref, norm_gain_ref, qkv_ref, lce_ref, out_w_ref, mlp_gain_ref, up_ref, down_ref,
     lines, straight, send, recv, keys_ref, values_ref, queries_ref, ctx_ref, combined,
+    scores_ref, peaks_ref, expons_ref, totals_ref, weights_ref,
     my_routes, all_routes, slots, slots_smem, place, place_smem, grid_v, padded,
     load_sem, send_sem, recv_sem, local_sem,
 ):
@@ -345,33 +346,53 @@
     factor = 32 ** (-0.5) / math.log(2)
     low_lanes = lax.broadcasted_iota(jnp.int32, (32, 128), 1) < 64
 
-    def attend(r, parity):
+    def gather(parts, r):
         base = (r // 8) * 32 + r % 8
-        found = [(p, place_smem[p, base + 8 * t]) for t in range(4) for p in range(4)]
-        keys = jnp.concatenate([keys_ref[p][s] for p, s in found], axis=0)
-        values = jnp.concatenate([values_ref[p][s] for p, s in found], axis=0)
-        scores = jnp.dot(keys, queries_ref[r], preferred_element_type=jnp.float32)
-        expons = jnp.exp2((scores - jnp.max(scores, axis=0, keepdims=True)) * factor)
-        weights = expons * (1.0 / jnp.sum(expons, axis=0, keepdims=True))
+        return jnp.concatenate(
+            [parts[p][place_smem[p, base + 8 * t]] for t in range(4) for p in range(4)], axis=0
+        )
+
+    def score(r, j):
+        scores = jnp.dot(gather(keys_ref, r), queries_ref[r], preferred_element_type=jnp.float32)
+        scores_ref[j][...] = scores
+        peaks_ref[j][...] = jnp.max(scores, axis=0, keepdims=True)
+
+    def soften(j):
+        expons = jnp.exp2((scores_ref[j][...] - peaks_ref[j][...]) * factor)
+        expons_ref[j][...] = expons
+        totals_ref[j][...] = jnp.sum(expons, axis=0, keepdims=True)
+
+    def weigh(j):
+        scale = 1.0 / totals_ref[j][...]
+        weights_ref[j][...] = (expons_ref[j][...] * scale).astype(jnp.bfloat16)
+
+    def blend(r, j):
         blended = lax.dot_general(
-            values, weights.astype(jnp.bfloat16), over_first, preferred_element_type=jnp.float32
+            gather(values_ref, r), weights_ref[j][...], over_first,
+            preferred_element_type=jnp.float32,
         )
         parts = []
         for h in range(HEADS):
-            part = blended[32 * h : 32 * h + 32, 128 * (h // 2) : 128 * (h // 2) + 128]
-            if h % 2 != parity:
-                part = pltpu.roll(part, 64, 1)
-            parts.append(part)
+            half = slice(128 * (h // 2), 128 * (h // 2) + 128)
+            part = blended[32 * h : 32 * h + 32, half]
+            parts.append(pltpu.roll(part, 64, 1) if h % 2 != j % 2 else part)
         return parts
 
-    @pl.loop(0, 32 // GROUP)
+    @pl.loop(0, 32 // GROUP + 3)
     def _(g):
-        for p in range(GROUP // 2):
-            r = g * GROUP + 2 * p
-            even, odd = attend(r, 0), attend(r + 1, 1)
+        done = jnp.maximum(g - 3, 0) * GROUP
+        for j in range(0, GROUP, 2):
+            even, odd = blend(done + j, j), blend(done + j + 1, j + 1)
             both = jnp.concatenate([jnp.where(low_lanes, a, b) for a, b in zip(even, odd)], axis=0)
-            attended = both.T.reshape(2, 64, 128)
-            combined[pl.ds(r, 2)] = (attended + ctx_ref[pl.ds(r, 2)]).astype(jnp.bfloat16)
+            attended = both.T.reshape(2, 64, 128) + ctx_ref[pl.ds(done + j, 2)]
+            combined[pl.ds(done + j, 2)] = attended.astype(jnp.bfloat16)
+        for j in range(GROUP):
+            weigh(j)
+        for j in range(GROUP):
+            soften(j)
+        ahead = jnp.minimum(g, 32 // GROUP - 1) * GROUP
+        for j in range(GROUP):
+            score(ahead + j, j)
 
     @pl.loop(0, 4)
     def _(i):
@@ -397,7 +418,7 @@
     wait_bytes(send[3], send_sem.at[8])
 
 
-GROUP = 8
+GROUP = 4
 
 
 def body(
@@ -425,6 +446,11 @@
             pltpu.VMEM((32, 128, 256), bf16),
             pltpu.VMEM((32, 64, 128), f32),
             pltpu.VMEM((32, 64, 128), bf16),
+            [pltpu.VMEM((256, 256), f32)] * GROUP,
+            [pltpu.VMEM((1, 256), f32)] * GROUP,
+            [pltpu.VMEM((256, 256), f32)] * GROUP,
+            [pltpu.VMEM((1, 256), f32)] * GROUP,
+            [pltpu.VMEM((256, 256), bf16)] * GROUP,
             pltpu.VMEM((1, 128), i32),
             pltpu.VMEM((128, 128), i32),
             pltpu.VMEM((24, 128), i32),

time: 74.3 us -> 68.2 us (0.918)
  Pallas kernels: 73.4 us -> 67.3 us
    pallas_call x1, Pallas kernels: 73.4 us -> 67.3 us  [body(): pl.pallas_call(block_kernel, out_shape=jax.ShapeDtypeStruct((32, 64, 128)...]
where the time goes in v4:
time: 68.2 us; the launch traced here: 68.1 us
  Pallas kernels  67.3 us (99%)
  local copies, waits for them, and re-layouts  0.8 us (1%)
    pallas_call x1, Pallas kernels, body(): pl.pallas_call(block_kernel, out_shape=jax.ShapeDtypeStruct((32, 64, 128)...  67.3 us

profile of v4, /device:TPU:1, one launch (start us, length us, event | category | flops | bytes accessed | tf_op | source)
XLA Modules:
  0.0 68.1 jit_solution(8534299017621095751)
XLA Ops:
  0.0 67.3 %block.1 = bf16[32,64,128]{2,1,0:T(8,128)(2,1)S(1)} custom-call(bf16[32,64,128]{2,1,0:T(8,128)(2,1)} %image_hbm.1, s32[4,4,8]{2,1,0:T(4,128)} %bitcast.3, f32[1,128]{1,0:T(1,128)} %bitcast.4, bf16[128,384]{1,0:T(8,128)(2,1)} %qkv_hbm.1, f32[5,5,128]{2,1,0:T(8,128)} %lce_hbm.1, bf16[128,128]{1,0:T(8,128)(2,1)} %out_w_hbm.1, f32[1,128]{1,0:T(1,128)} %bitcast.5, ...), custom_call_target="tpu_custom_call" | custom-call | tf_op jit(solution)/shard_map/block/pallas_call | solution.py:434
  67.3 0.8 %copy.11 = bf16[32,64,128]{2,1,0:T(8,128)(2,1)} copy(bf16[32,64,128]{2,1,0:T(8,128)(2,1)S(1)} %block.1) | data formatting | bytes 1048576

commit v5 on v4

--- a/solution.py
+++ b/solution.py
@@ -28,7 +28,9 @@
 PLANE = sorted(
     (o for o in itertools.product(range(2), range(4), range(4)) if any(o)), key=hops
 )
-BATCHES = (range(0, 8), range(8, 16), range(16, 22), range(22, 27), range(27, 31))
+BATCHES = (
+    range(0, 8), range(8, 16), range(16, 22), range(22, 26), range(26, 29), range(29, 31)
+)
 BATCH_OF = [b for b, members in enumerate(BATCHES) for _ in members]
 
 
@@ -61,7 +63,7 @@
     image_ref, routes_ref, norm_gain_ref, qkv_ref, lce_ref, out_w_ref, mlp_gain_ref, up_ref, down_ref,
     lines, straight, send, recv, keys_ref, values_ref, queries_ref, ctx_ref, combined,
     scores_ref, peaks_ref, expons_ref, totals_ref, weights_ref,
-    my_routes, all_routes, slots, slots_smem, place, place_smem, grid_v, padded,
+    my_routes, all_routes, slots, slots_smem, place, place_smem, grid_v, padded, edge_rows, edge_send, edge_recv,
     load_sem, send_sem, recv_sem, local_sem,
 ):
     row, col = lax.axis_index("rows"), lax.axis_index("cols")
@@ -116,6 +118,10 @@
         )
         values = values.reshape(8, 8, 8, 128).transpose(1, 0, 2, 3)
         grid_v[pl.ds(2 + 8 * i, 8), pl.ds(1, 8)] = values.astype(jnp.bfloat16)
+        for t in range(8):
+            edge_rows[0, pl.ds(16 * i + 2 * t, 2), :] = values[t, 0, 0:2, :]
+            edge_rows[1, pl.ds(16 * i + 2 * t, 2), :] = values[t, 7, 6:8, :]
+    edge_send[...] = edge_rows[...].astype(jnp.bfloat16)
 
     lanes = lax.broadcasted_iota(jnp.int32, (128, 128), 1)
     subs = lax.broadcasted_iota(jnp.int32, (128, 128), 0)
@@ -151,12 +157,17 @@
     for n, (dr, dc) in enumerate(
         (dr, dc) for dr in (-1, 0, 1) for dc in (-1, 0, 1) if (dr, dc) != (0, 0)
     ):
-        rows = {-1: (2, 34, 2), 0: (2, 2, 32), 1: (32, 0, 2)}[dr]
-        cols = {-1: (1, 9, 1), 0: (1, 1, 8), 1: (8, 0, 1)}[dc]
+        if dr == 0:
+            source, sink = edge_send.at[(dc + 1) // 2], edge_recv.at[(1 - dc) // 2]
+        else:
+            rows = {-1: (2, 34), 1: (32, 0)}[dr]
+            cols = {-1: (1, 9, 1), 0: (1, 1, 8), 1: (8, 0, 1)}[dc]
+            source = grid_v.at[pl.ds(rows[0], 2), pl.ds(cols[0], cols[2])]
+            sink = grid_v.at[pl.ds(rows[1], 2), pl.ds(cols[1], cols[2])]
         halo_copies.append(
             pltpu.make_async_remote_copy(
-                src_ref=grid_v.at[pl.ds(rows[0], rows[2]), pl.ds(cols[0], cols[2])],
-                dst_ref=grid_v.at[pl.ds(rows[1], rows[2]), pl.ds(cols[1], cols[2])],
+                src_ref=source,
+                dst_ref=sink,
                 send_sem=send_sem.at[1],
                 recv_sem=recv_sem.at[1 + n],
                 device_id=((row + dr + 8) % 8, (col + dc + 16) % 16),
@@ -289,13 +300,18 @@
         inside = jnp.logical_and(
             jnp.logical_or(i >= 2, keep_top), jnp.logical_or(i < 34, keep_bottom)
         )
-        for j in range(10):
-            keep = inside
-            if j == 0:
-                keep = jnp.logical_and(inside, keep_left)
-            if j == 9:
-                keep = jnp.logical_and(inside, keep_right)
-            padded[i, pl.ds(8 * j, 8), :] = jnp.where(keep, grid_v[i, j].astype(jnp.float32), 0.0)
+        for j in range(1, 9):
+            padded[i, pl.ds(8 * j, 8), :] = jnp.where(inside, grid_v[i, j].astype(jnp.float32), 0.0)
+
+    for j, keep in ((0, keep_left), (9, keep_right)):
+        for i, also in ((0, keep_top), (1, keep_top), (34, keep_bottom), (35, keep_bottom)):
+            padded[i, pl.ds(8 * j, 8), :] = jnp.where(
+                jnp.logical_and(keep, also), grid_v[i, j].astype(jnp.float32), 0.0
+            )
+    for side, keep in ((0, keep_left), (1, keep_right)):
+        edge_rows[side] = jnp.where(keep, edge_recv[side].astype(jnp.float32), 0.0)
+        for i in range(32):
+            padded[2 + i, pl.ds((6, 72)[side], 2), :] = edge_rows[side, pl.ds(2 * i, 2), :]
 
     @pl.loop(0, 8)
     def _(j):
@@ -378,24 +394,30 @@
             parts.append(pltpu.roll(part, 64, 1) if h % 2 != j % 2 else part)
         return parts
 
-    @pl.loop(0, 32 // GROUP + 3)
-    def _(g):
-        done = jnp.maximum(g - 3, 0) * GROUP
-        for j in range(0, GROUP, 2):
-            even, odd = blend(done + j, j), blend(done + j + 1, j + 1)
-            both = jnp.concatenate([jnp.where(low_lanes, a, b) for a, b in zip(even, odd)], axis=0)
-            attended = both.T.reshape(2, 64, 128) + ctx_ref[pl.ds(done + j, 2)]
-            combined[pl.ds(done + j, 2)] = attended.astype(jnp.bfloat16)
-        for j in range(GROUP):
-            weigh(j)
-        for j in range(GROUP):
-            soften(j)
-        ahead = jnp.minimum(g, 32 // GROUP - 1) * GROUP
-        for j in range(GROUP):
-            score(ahead + j, j)
-
-    @pl.loop(0, 4)
-    def _(i):
+    def step(g):
+        if g >= 3:
+            done = (g - 3) * GROUP
+            for j in range(0, GROUP, 2):
+                even, odd = blend(done + j, j), blend(done + j + 1, j + 1)
+                both = jnp.concatenate(
+                    [jnp.where(low_lanes, a, b) for a, b in zip(even, odd)], axis=0
+                )
+                attended = both.T.reshape(2, 64, 128) + ctx_ref[pl.ds(done + j, 2)]
+                combined[pl.ds(done + j, 2)] = attended.astype(jnp.bfloat16)
+        if 2 <= g < STEPS + 2:
+            for j in range(GROUP):
+                weigh(j)
+        if 1 <= g < STEPS + 1:
+            for j in range(GROUP):
+                soften(j)
+        if g < STEPS:
+            for j in range(GROUP):
+                score(g * GROUP + j, j)
+
+    for g in range(STEPS + 3):
+        step(g)
+
+    def finish(i):
         strip = to_strip(image_ref[pl.ds(8 * i, 8)].astype(jnp.float32)).reshape(512, 128)
         mixed = jnp.dot(
             combined[pl.ds(8 * i, 8)].reshape(512, 128), out_w_ref[...],
@@ -409,6 +431,9 @@
         refined = (stored + lowered).reshape(8, 64, 128)
         refined_ref[pl.ds(8 * i, 8)] = to_strip(refined).astype(jnp.bfloat16)
 
+    for i in range(4):
+        finish(i)
+
     wait_bytes(all_routes.at[pl.ds(0, 127)], send_sem.at[0])
     for copy in halo_copies:
         wait_bytes(copy.src_ref, send_sem.at[1])
@@ -419,6 +444,7 @@
 
 
 GROUP = 4
+STEPS = 32 // GROUP
 
 
 def body(
@@ -459,6 +485,9 @@
             pltpu.SMEM((4, 128), i32),
             pltpu.VMEM((36, 10, 8, 128), bf16),
             pltpu.VMEM((36, 80, 128), f32),
+            pltpu.VMEM((2, 64, 128), f32),
+            pltpu.VMEM((2, 64, 128), bf16),
+            pltpu.VMEM((2, 64, 128), bf16),
             dma((9,)), dma((9,)), dma((13 + 3 * len(BATCHES),)), dma((2,)),
         ],
         compiler_params=pltpu.CompilerParams(

time: 68.2 us -> 62.6 us (0.918); the launches traced: 68.1 us -> 61.8 us
  Pallas kernels: 67.3 us -> 60.9 us
    pallas_call x1, Pallas kernels: 67.3 us -> 60.9 us  [body(): pl.pallas_call(block_kernel, out_shape=jax.ShapeDtypeStruct((32, 64, 128)...]
where the time goes in v5:
time: 62.6 us; the launch traced here: 61.8 us
  Pallas kernels  60.9 us (97%)
  local copies, waits for them, and re-layouts  0.8 us (1%)
    pallas_call x1, Pallas kernels, body(): pl.pallas_call(block_kernel, out_shape=jax.ShapeDtypeStruct((32, 64, 128)...  60.9 us

profile of v5, /device:TPU:1, one launch (start us, length us, event | category | flops | bytes accessed | tf_op | source)
XLA Modules:
  0.0 61.8 jit_solution(5627494953587067708)
XLA Ops:
  0.0 60.9 %block.1 = bf16[32,64,128]{2,1,0:T(8,128)(2,1)S(1)} custom-call(bf16[32,64,128]{2,1,0:T(8,128)(2,1)} %image_hbm.1, s32[4,4,8]{2,1,0:T(4,128)} %bitcast.3, f32[1,128]{1,0:T(1,128)} %bitcast.4, bf16[128,384]{1,0:T(8,128)(2,1)} %qkv_hbm.1, f32[5,5,128]{2,1,0:T(8,128)} %lce_hbm.1, bf16[128,128]{1,0:T(8,128)(2,1)} %out_w_hbm.1, f32[1,128]{1,0:T(1,128)} %bitcast.5, ...), custom_call_target="tpu_custom_call" | custom-call | tf_op jit(solution)/shard_map/block/pallas_call | solution.py:460
  61.0 0.8 %copy.11 = bf16[32,64,128]{2,1,0:T(8,128)(2,1)} copy(bf16[32,64,128]{2,1,0:T(8,128)(2,1)S(1)} %block.1) | data formatting | bytes 1048576

commit v6 on v5

--- a/solution.py
+++ b/solution.py
@@ -153,6 +153,22 @@
         )
         route_copies[-1].start()
 
+    line_copies = []
+    for p in range(3):
+        for step in (2, 1, 3):
+            offset = tuple(step if axis == 3 - (0, 2, 1)[p] else 0 for axis in range(4))
+            line_copies.append(
+                pltpu.make_async_remote_copy(
+                    src_ref=lines[p].at[spots[p]],
+                    dst_ref=lines[p].at[spots[p]],
+                    send_sem=send_sem.at[2 + p],
+                    recv_sem=recv_sem.at[9 + p],
+                    device_id=peer(offset),
+                    device_id_type=MESH,
+                )
+            )
+            line_copies[-1].start()
+
     halo_copies = []
     for n, (dr, dc) in enumerate(
         (dr, dc) for dr in (-1, 0, 1) for dc in (-1, 0, 1) if (dr, dc) != (0, 0)
@@ -175,22 +191,6 @@
             )
         )
         halo_copies[-1].start()
-
-    line_copies = []
-    for p in range(3):
-        for step in (1, 3, 2):
-            offset = tuple(step if axis == 3 - (0, 2, 1)[p] else 0 for axis in range(4))
-            line_copies.append(
-                pltpu.make_async_remote_copy(
-                    src_ref=lines[p].at[spots[p]],
-                    dst_ref=lines[p].at[spots[p]],
-                    send_sem=send_sem.at[2 + p],
-                    recv_sem=recv_sem.at[9 + p],
-                    device_id=peer(offset),
-                    device_id_type=MESH,
-                )
-            )
-            line_copies[-1].start()
 
     query_w = qkv_ref[:, 0:128].T
     feature_head = lax.broadcasted_iota(jnp.int32, (128, 256), 0) // 32

time: 62.6 us -> 64.4 us (1.029); the launches traced: 61.8 us -> 64.2 us
  Pallas kernels: 60.9 us -> 63.4 us
    pallas_call x1, Pallas kernels: 60.9 us -> 63.4 us  [body(): pl.pallas_call(block_kernel, out_shape=jax.ShapeDtypeStruct((32, 64, 128)...]
where the time goes in v6:
time: 64.4 us; the launch traced here: 64.2 us
  Pallas kernels  63.4 us (98%)
  local copies, waits for them, and re-layouts  0.8 us (1%)
    pallas_call x1, Pallas kernels, body(): pl.pallas_call(block_kernel, out_shape=jax.ShapeDtypeStruct((32, 64, 128)...  63.4 us

profile of v6, /device:TPU:1, one launch (start us, length us, event | category | flops | bytes accessed | tf_op | source)
XLA Modules:
  0.0 64.2 jit_solution(7473327353065589569)
XLA Ops:
  0.0 63.4 %block.1 = bf16[32,64,128]{2,1,0:T(8,128)(2,1)S(1)} custom-call(bf16[32,64,128]{2,1,0:T(8,128)(2,1)} %image_hbm.1, s32[4,4,8]{2,1,0:T(4,128)} %bitcast.3, f32[1,128]{1,0:T(1,128)} %bitcast.4, bf16[128,384]{1,0:T(8,128)(2,1)} %qkv_hbm.1, f32[5,5,128]{2,1,0:T(8,128)} %lce_hbm.1, bf16[128,128]{1,0:T(8,128)(2,1)} %out_w_hbm.1, f32[1,128]{1,0:T(1,128)} %bitcast.5, ...), custom_call_target="tpu_custom_call" | custom-call | tf_op jit(solution)/shard_map/block/pallas_call | solution.py:460
  63.4 0.8 %copy.11 = bf16[32,64,128]{2,1,0:T(8,128)(2,1)} copy(bf16[32,64,128]{2,1,0:T(8,128)(2,1)S(1)} %block.1) | data formatting | bytes 1048576
